TPU v7x, 32 devices: a whole 2x2x4 slice. The times are simulated.
32 devices in a mesh: gx: 8 (over z, y), gy: 4 (over x, core).
Axes of the slice: x: 2, y: 2, z: 4, core: 2. Of those that a mesh axis runs over, the one named last changes fastest.
Arguments:
- vorticity_grid: float32 [4096, 4096], P(('gx', 'gy')), may hold values from -6 to 6
- forcing_grid: float32 [4096, 4096], P(('gx', 'gy')), may hold values from -12 to 12
- cutoff: int32 [1], replicated, may hold values from 853 to 1365
- forcing_shells: int32 [4], replicated, may hold values from 2 to 127
Outputs:
- lifted_spectrum: float32 [2, 4096, 4096], P(None, ('gx', 'gy'))
- coarse_field: float32 [256, 256], P(('gx', 'gy'))
Inputs may be any that keep to these rules, and one draw needn't show every extreme that they name: Nonlinear modes with an absolute wavenumber index above cutoff are removed.
All inputs are finite; a program needn't handle non-finite values.
Results may differ from a plain program's by a relative error of at most 0.0001.
Values sent between devices are 32-bit elements; how exact they have to be, the bound alone decides.
A program may use at most 128 MiB of HBM per device.

v0:
```python
import math

import jax
import jax.numpy as jnp
import numpy as np
from jax import lax
from jax.sharding import PartitionSpec as P

LOW = 256
SHELLS = 4
AXES = ("gx", "gy")

time_step = 0.05
viscosity = 0.05
coarse_ratio = 4.0


def contract(pattern, left_side, right_side):
    return jnp.einsum(pattern, left_side, right_side, precision=lax.Precision.HIGH)


def turn(product, length_of):
    phases = 2.0 * np.pi / length_of * (product % length_of)
    return np.cos(phases), np.sin(phases)


def rotation(cos_part, sin_part, axes):
    pairs = np.stack([np.stack([cos_part, -sin_part]), np.stack([sin_part, cos_part])])
    return np.moveaxis(pairs, (0, 1), axes).astype(np.float32)


def wave_tables(grid, total, rows):
    A = max(64, total)
    B = grid // A
    half = B // 2
    scale = 1.0 / math.sqrt(grid)
    k, a = np.arange(A), np.arange(A)
    b, j = np.arange(B), np.arange(half)
    out = {"A": A, "B": B, "half": half}
    cos_t, sin_t = turn(k[:, None] * a[None, :], A)
    out["y1"] = np.stack([cos_t, -sin_t], 1).astype(np.float32)
    out["kb"] = np.stack(turn(k[:, None] * b[None, :], grid)).astype(np.float32)
    out["jb"] = np.stack(turn(j[:, None] * b[None, :], B)).astype(np.float32)
    cos_t, sin_t = turn(a[:, None] * k[None, :], A)
    out["iy1"] = np.stack([cos_t, -sin_t], 2).astype(np.float32)
    p, s = np.arange(total), np.arange(total)
    q, lane = np.arange(rows), np.arange(rows)
    cos_t, sin_t = turn(p[:, None] * s[None, :], total)
    out["x1"] = rotation(cos_t * scale, -sin_t * scale, (1, 3))
    out["ix1"] = rotation(cos_t.T * scale, sin_t.T * scale, (1, 3))
    cos_t, sin_t = turn(q[:, None] * lane[None, :], rows)
    out["x2"] = rotation(cos_t.T, -sin_t.T, (2, 0))
    out["ix2"] = rotation(cos_t, sin_t, (2, 0))
    cos_t, sin_t = turn(p[:, None] * lane[None, :], grid)
    out["tw"] = np.stack([cos_t, sin_t]).astype(np.float32)
    return out


def second_tables(tables, grid):
    scale = 1.0 / math.sqrt(grid)
    kb, jb = lax.optimization_barrier((tables["kb"], tables["jb"]))
    k = lax.broadcasted_iota(jnp.int32, (tables["A"], 1, 1, 1, 1), 0)

    def multiplied(left, right):
        return (left[0] * right[0] - left[1] * right[1], left[1] * right[0] + left[0] * right[1])

    def paired(cos_part, sin_part):
        to_real = jnp.stack([cos_part, -sin_part], 2)
        to_imag = jnp.stack([sin_part, cos_part], 2)
        return jnp.stack([to_real, to_imag], 1)

    half, width = tables["half"], tables["B"]
    sign = scale * (1.0 - 2.0 * (lax.iota(jnp.int32, width) % 2).astype(jnp.float32))
    d = lax.broadcasted_iota(jnp.int32, (1, 2, 1, 1, 1), 1)
    cos_t, sin_t = multiplied(kb[:, :, None, :], jb[:, None, :, :])
    plain = paired(scale * cos_t, -scale * sin_t)
    j = lax.broadcasted_iota(jnp.int32, (1, 1, half, 1, 1), 2)
    c = lax.broadcasted_iota(jnp.int32, (1, 1, 1, 2, 1), 3)
    riding = jnp.where(c == 0, sign[None, None, None, None, :], 0.0)
    table = jnp.where((k == 0) & (d == 1) & (j == 0), riding, plain)
    cos_t, sin_t = multiplied(kb[:, :, :, None], jb.swapaxes(1, 2)[:, None])
    ky = k[:, :, :, 0, 0] + tables["A"] * lax.broadcasted_iota(jnp.int32, (1, 1, half), 2)
    weight = jnp.where(ky == 0, scale, 2.0 * scale)
    slope = ky.astype(jnp.float32) * (2.0 * math.pi / grid) * weight
    back = paired(cos_t * weight, sin_t * weight)
    j = lax.broadcasted_iota(jnp.int32, (1, 1, 1, 1, half), 4)
    riding = jnp.where(d == 0, sign[None, None, :, None, None], 0.0)
    back = jnp.where((k == 0) & (c == 1) & (j == 0), riding, back)
    back_slope = paired(-sin_t * slope, cos_t * slope)
    return {"y2": table, "y2_plain": plain, "iy": back, "iyd": back_slope}


def body(vorticity_grid, forcing_grid, cutoff, forcing_shells):
    rows, grid = vorticity_grid.shape
    total = lax.axis_size("gx") * lax.axis_size("gy")
    rank = lax.axis_index("gx") * lax.axis_size("gy") + lax.axis_index("gy")
    tables = wave_tables(grid, total, rows)
    tables.update(second_tables(tables, grid))
    A, B, half = tables["A"], tables["B"], tables["half"]
    local = A // total
    half_low = LOW // 2
    kept = (grid // 3) // A + 1
    driven = -(-half_low // A)
    unit = 2.0 * math.pi / grid

    def exchange(values):
        return lax.all_to_all(values, AXES, split_axis=0, concat_axis=0, tiled=True)

    def forward_y(fields, table):
        first = contract("kda,abx->kdbx", tables["y1"], fields)
        second = contract("kdjcb,kcbx->kdjx", table, first)
        return second.reshape((total, local) + second.shape[1:])

    def inverse_y(waves, table):
        waves = waves.reshape((A,) + waves.shape[2:])
        first = contract("kdbcj,kcjx->kdbx", table[..., : waves.shape[2]], waves)
        return contract("akd,kdbx->abx", tables["iy1"], first)

    def twiddle(values, direction):
        cos_t = tables["tw"][0][:, None, None, :]
        sin_t = direction * tables["tw"][1][:, None, None, :]
        real, imag = values[:, :, 0], values[:, :, 1]
        return jnp.stack([real * cos_t - imag * sin_t, real * sin_t + imag * cos_t], 2)

    def forward_x(waves):
        first = contract("pdsc,skcjl->pkdjl", tables["x1"], waves)
        return contract("pkcjl,cldq->pkdjq", twiddle(first, -1.0), tables["x2"])

    def inverse_x(waves):
        first = contract("pkcjq,cqdl->pkdjl", waves, tables["ix2"])
        return contract("sdpc,pkcjl->skdjl", tables["ix1"], twiddle(first, 1.0))

    p_ids = jnp.arange(total, dtype=jnp.int32)[:, None, None, None]
    q_ids = jnp.arange(rows, dtype=jnp.int32)[None, None, None, :]
    k_ids = (rank * local + jnp.arange(local, dtype=jnp.int32))[None, :, None, None]
    j_ids = jnp.arange(half, dtype=jnp.int32)[None, None, :, None]
    kx_ids = p_ids + total * q_ids
    wave_x = jnp.where(kx_ids < grid // 2, kx_ids, kx_ids - grid)
    deriv_x = jnp.where(kx_ids == grid // 2, 0, wave_x).astype(jnp.float32) * unit
    wave_y = k_ids + A * j_ids
    nyquist_y = jnp.full((1, 1, 1, 1), -(grid // 2), jnp.int32)
    origin = (k_ids == 0) & (j_ids == 0)

    def laplacian(rows_y):
        return (wave_x * wave_x + rows_y * rows_y).astype(jnp.float32) * (unit * unit)

    def inverse_laplacian(rows_y):
        squares = wave_x * wave_x + rows_y * rows_y
        lap = squares.astype(jnp.float32) * (unit * unit)
        return jnp.where(squares == 0, 0.0, 1.0 / jnp.maximum(lap, unit * unit))

    def slope_x(pair):
        return (-deriv_x * pair[1], deriv_x * pair[0])

    def packed(main, extra):
        real, imag = main
        if extra is not None:
            real = jnp.where(origin, real - extra[1], real)
            imag = jnp.where(origin, imag + extra[0], imag)
        return jnp.stack([real, imag], 2)

    turned = vorticity_grid.T.reshape(A, B, rows)
    start_half = forward_y(turned, tables["y2"])
    force_half = forward_y(
        forcing_grid.T.reshape(A, B, rows), tables["y2_plain"][:, :, :driven]
    )
    moved = exchange(jnp.concatenate([start_half, force_half], 3))
    spectra = forward_x(moved)
    state = (spectra[:, :, 0, :half], spectra[:, :, 1, :half])
    squares = (wave_x * wave_x + wave_y * wave_y)[:, :, :driven]
    shell = jnp.zeros(squares.shape, bool)
    for index in range(SHELLS):
        radius = forcing_shells[index]
        shell = shell | ((radius * radius <= squares) & (squares < (radius + 1) * (radius + 1)))
    drive = tuple(jnp.where(shell, spectra[:, :, c, half:], 0.0) for c in (0, 1))

    def mirrored(natural):
        return jnp.roll(jnp.flip(natural, -1), 1, -1)

    zero_real, zero_imag = state[0][:, 0, 0].T.reshape(grid), state[1][:, 0, 0].T.reshape(grid)
    back_real, back_imag = mirrored(zero_real), -mirrored(zero_imag)
    own_real, own_imag = 0.5 * (zero_real + back_real), 0.5 * (zero_imag + back_imag)
    nyq_real, nyq_imag = 0.5 * (zero_imag - back_imag), -0.5 * (zero_real - back_real)

    def laid(natural):
        return natural.reshape(rows, total).T[:, None, None, :]

    state = tuple(
        jnp.where(origin, laid(own), part) for own, part in zip((own_real, own_imag), state)
    )
    extra = (laid(nyq_real), laid(nyq_imag))
    lap, inv_lap = laplacian(wave_y), inverse_laplacian(wave_y)
    lap_n, inv_lap_n = laplacian(nyquist_y), inverse_laplacian(nyquist_y)
    dealias = ((jnp.abs(wave_x) <= cutoff[0]) & (jnp.abs(wave_y) <= cutoff[0]))[:, :, :kept]

    def widened(part, count):
        return jnp.pad(part, ((0, 0), (0, 0), (0, count - part.shape[2]), (0, 0)))

    drive_kept = tuple(widened(part, kept) for part in drive)

    def product(psi, psi_x, vort, vort_x):
        speed_u = inverse_y(psi, tables["iyd"])
        slope_wx = inverse_y(vort_x, tables["iy"])
        speed_v = -inverse_y(psi_x, tables["iy"])
        slope_wy = inverse_y(vort, tables["iyd"])
        advect = speed_u * slope_wx + speed_v * slope_wy
        term = forward_x(exchange(forward_y(advect, tables["y2_plain"][:, :, :kept])))
        return tuple(
            drive_kept[c] - jnp.where(dealias, term[:, :, c], 0.0) for c in (0, 1)
        )

    psi = tuple(inv_lap * part for part in state)
    psi_extra = tuple(inv_lap_n * part for part in extra)
    outgoing = jnp.concatenate(
        [
            packed(psi, psi_extra),
            packed(slope_x(psi), slope_x(psi_extra)),
            packed(slope_x(state), slope_x(extra)),
        ],
        3,
    )
    arrived = exchange(inverse_x(outgoing))
    psi_half = arrived[:, :, :, :half]
    psi_x_half = arrived[:, :, :, half : 2 * half]
    vort_x_half = arrived[:, :, :, 2 * half :]
    first = product(psi_half, psi_x_half, start_half, vort_x_half)

    moved_on = tuple(
        part - time_step * viscosity * lap * part + time_step * widened(term, half)
        for part, term in zip(state, first)
    )
    moved_extra = tuple(part - time_step * viscosity * lap_n * part for part in extra)
    psi_kept = tuple(time_step * inv_lap[:, :, :kept] * term for term in first)
    outgoing = jnp.concatenate(
        [
            packed(moved_on, moved_extra),
            packed(slope_x(moved_on), slope_x(moved_extra)),
            jnp.stack(psi_kept, 2),
            jnp.stack(slope_x(psi_kept), 2),
        ],
        3,
    )
    arrived = exchange(inverse_x(outgoing))

    def added(whole, local_part, part):
        part = jnp.pad(part, ((0, 0), (0, 0), (0, 0), (0, half - kept), (0, 0)))
        return whole - time_step * viscosity * local_part + part

    second = product(
        added(psi_half, start_half, arrived[:, :, :, 2 * half : 2 * half + kept]),
        added(psi_x_half, vort_x_half, arrived[:, :, :, 2 * half + kept :]),
        arrived[:, :, :, :half],
        arrived[:, :, :, half : 2 * half],
    )

    def stepped(part, ahead, lap_of, terms):
        linear = -viscosity * lap_of * (part + ahead)
        return part + 0.5 * time_step * (linear if terms is None else linear + terms)

    final = tuple(
        stepped(part, ahead, lap, widened(one + two, half))
        for part, ahead, one, two in zip(state, moved_on, first, second)
    )
    final_extra = tuple(
        stepped(part, ahead, lap_n, None) for part, ahead in zip(extra, moved_extra)
    )
    projected = tuple(new + coarse_ratio * (new - old) for new, old in zip(final, state))

    def lifted(signed_x, signed_y):
        low = (
            (signed_x >= -half_low)
            & (signed_x < half_low)
            & (signed_y >= -half_low)
            & (signed_y < half_low)
        )
        return jnp.stack(
            [jnp.where(low, ahead, now) for ahead, now in zip(projected, final)], 2
        )

    straight = lifted(wave_x, wave_y)
    mirror = lifted(-wave_x, -wave_y)
    nyquist = jnp.stack([part[:, 0] for part in final_extra], 1)[:, None]
    flipped = jnp.flip(mirror, 3)
    shifted = jnp.concatenate(
        [jnp.broadcast_to(nyquist, flipped[:, :, :, :1].shape), flipped[:, :, :, :-1]], 3
    )
    flipped = jnp.where((k_ids == 0)[:, :, None], shifted, flipped)
    lanes = np.arange(rows)
    head_turn = (lanes[:, None] == (rows - lanes[None, :]) % rows).astype(np.float32)
    tail_turn = (lanes[:, None] == rows - 1 - lanes[None, :]).astype(np.float32)
    flipped = flipped * jnp.array([1.0, -1.0], jnp.float32)[None, None, :, None, None]
    highest = lax.Precision.HIGHEST
    head = jnp.einsum("pkdjq,qr->pkdjr", flipped[:1], head_turn, precision=highest)
    tail = jnp.einsum("pkdjq,qr->pkdjr", flipped[1:], tail_turn, precision=highest)
    flipped = jnp.concatenate([head, jnp.flip(tail, 0)], 0)
    whole = jnp.concatenate([straight, flipped], 3)
    backwards = rank >= total // 2
    if rows >= A:
        shape = (total, local, 2, total, rows // A, rows)
        sent = whole.reshape(shape).transpose(3, 1, 4, 2, 0, 5)
        block = exchange(sent).reshape(A, rows // A, 2, total, rows)
        block = jnp.where(backwards, jnp.roll(jnp.flip(block, 0), 1, 0), block)
        spectrum = block.transpose(2, 1, 0, 4, 3).reshape(2, rows, grid)
    else:
        parts = A // rows
        sent = whole.transpose(3, 1, 2, 0, 4)
        sent = jnp.broadcast_to(sent[:, None], (B, parts) + sent.shape[1:])
        block = exchange(sent.reshape((total,) + sent.shape[2:])).reshape(A, 2, total, rows)
        block = jnp.where(backwards, jnp.roll(jnp.flip(block, 0), 1, 0), block)
        block = lax.dynamic_slice_in_dim(block, (rank % parts) * rows, rows, 0)
        spectrum = block.transpose(1, 0, 3, 2).reshape(2, rows, grid)

    own = LOW // total
    block_ids = np.arange(LOW)
    col_cos, col_sin = (t.astype(np.float32) / 16.0 for t in turn(block_ids[:, None] * block_ids, LOW))
    low = jnp.concatenate([spectrum[:, :, :half_low], spectrum[:, :, grid - half_low :]], 2)
    column = np.stack([np.stack([col_cos, col_sin]), np.stack([-col_sin, col_cos])])
    mixed = contract("cqp,cdpa->dqa", low, column)
    mixed = mixed.reshape(2, rows, total, own).transpose(2, 0, 1, 3)
    mixed = exchange(mixed)
    count = -(-half_low // rows)
    mixed = jnp.concatenate([mixed[:count], mixed[total - count :]], 0)
    if rows * count != half_low:
        first_rows = mixed[:count].transpose(1, 0, 2, 3).reshape(2, count * rows, own)[:, :half_low]
        last_rows = mixed[count:].transpose(1, 0, 2, 3).reshape(2, count * rows, own)[:, -half_low:]
        mixed = jnp.concatenate([first_rows, last_rows], 1)
    else:
        mixed = mixed.transpose(1, 0, 2, 3).reshape(2, LOW, own)
    row_table = np.stack([col_cos, -col_sin])
    coarse = contract("cqa,cqb->ab", mixed, row_table)
    return (spectrum, coarse)


def solution(mesh):
    placed = (P(AXES, None), P(AXES, None), P(), P())
    return jax.shard_map(
        body,
        mesh=mesh,
        in_specs=placed,
        out_specs=(P(None, AXES, None), P(AXES, None)),
        check_vma=False,
    )
```

profile of v0, /device:TPU:0, one launch (start us, length us, event | category | flops | bytes accessed | tf_op | source)
XLA Modules:
  0.0 820.7 jit_solution(10306292651187544082)
XLA Ops:
  7.0 4.5 convolution_bitcast_fusion.7
  15.7 4.1 fusion.16
  19.8 5.4 fusion.9
  29.0 7.3 all-to-all-start
  37.8 50.1 %all-to-all-done = f32[32,2,2,34,128]{4,2,3,1,0:T(2,128)S(1)} async-done(((f32[32,2,2,34,128]{4,2,3,1,0:T(2,128)}), f32[32,2,2,34,128]{4,2,3,1,0:T(2,128)S(1)}, u32[]{:S(2)}, u32[]{:S(2)}) %all-to-all-start) | async-done | bytes 2228256 | tf_op jit(solution)/shard_map/all_to_all | solution.py:107
  106.4 5.9 fusion.50
  114.4 6.9 fusion.53
  121.3 7.5 copy.139
  128.8 4.4 all-to-all-start.1
  137.6 3.6 convolution_bitcast_fusion.4
  141.1 4.9 fusion.27
  146.1 127.0 %all-to-all-done.1 = f32[32,2,2,96,128]{4,2,3,1,0:T(2,128)} async-done(((f32[32,2,2,96,128]{4,2,3,1,0:T(2,128)}), f32[32,2,2,96,128]{4,2,3,1,0:T(2,128)}, u32[]{:S(2)}, u32[]{:S(2)}) %all-to-all-start.1) | async-done | bytes 6291488 | tf_op jit(solution)/shard_map/all_to_all | solution.py:107
  273.0 3.3 fusion.185
  279.6 3.6 convolution_bitcast_fusion.5
  283.2 3.6 fusion.33
  289.1 4.2 fusion.60
  293.3 4.1 fusion.31
  297.7 4.2 fusion.63
  301.9 3.7 fusion.29
  307.8 4.4 fusion.14
  332.6 19.2 %all-to-all-done.2 = f32[32,2,2,22,128]{4,2,3,1,0:T(2,128)S(1)} async-done(((f32[32,2,2,22,128]{4,2,3,1,0:T(2,128)}), f32[32,2,2,22,128]{4,2,3,1,0:T(2,128)S(1)}, u32[]{:S(2)}, u32[]{:S(2)}) %all-to-all-start.2) | async-done | bytes 1441824 | tf_op jit(solution)/shard_map/all_to_all | solution.py:107
  361.3 3.0 fusion.44
  366.4 8.7 %fusion.47 = f32[32,2,2,108,128]{4,0,2,3,1:T(8,128)} fusion(f32[32,2,32,2,1,1]{2,0,3,1,5,4:T(8,128)S(1)} %copy-done.55, f32[32,2,2,108,128,1]{4,3,2,1,0,5:T(8,128)S(1)} %maximum_bitcast_fusion.1), kind=kOutput, calls=%fused_computation.62 | convolution fusion | flops 679477248 | bytes 14172160 | tf_op jit(solution)/shard_map/sdpc,pkcjl->skdjl/dot_general | solution.py:19
  375.2 11.3 %copy.155 = f32[32,2,2,108,128]{4,2,3,1,0:T(2,128)} copy(f32[32,2,2,108,128]{4,0,2,3,1:T(8,128)} %fusion.47) | data formatting | bytes 14155776 | tf_op jit(solution)/shard_map/sdpc,pkcjl->skdjl/transpose | solution.py:19
  386.5 159.0 %all_to_all.35 = f32[32,2,2,108,128]{4,2,3,1,0:T(2,128)S(1)} all-to-all(f32[32,2,2,108,128]{4,2,3,1,0:T(2,128)} %copy.155), channel_id=1, replica_groups=mesh['gx'=8,'gy'=4] {'gx','gy'}, dimensions={0} | all-to-all | bytes 14155776 | tf_op jit(solution)/shard_map/all_to_all | solution.py:107
  549.4 3.6 convolution_bitcast_fusion.2
  553.0 3.6 fusion.25
  559.5 4.4 fusion.66
  563.9 3.6 fusion.23
  569.8 4.2 fusion.69
  573.9 4.1 fusion.21
  578.3 3.6 convolution_bitcast_fusion.1
  582.0 3.6 fusion.19
  587.8 4.6 fusion.12
  594.3 3.7 all-to-all-start.4
  598.1 34.8 %all-to-all-done.4 = f32[32,2,2,22,128]{4,2,3,1,0:T(2,128)S(1)} async-done(((f32[32,2,2,22,128]{4,2,3,1,0:T(2,128)}), f32[32,2,2,22,128]{4,2,3,1,0:T(2,128)S(1)}, u32[]{:S(2)}, u32[]{:S(2)}) %all-to-all-start.4) | async-done | bytes 1441824 | tf_op jit(solution)/shard_map/all_to_all | solution.py:107
  642.5 4.0 slice.253
  654.4 3.2 rev.14
  660.0 4.4 copy.399
  664.5 4.0 all-to-all-start.5
  668.5 93.7 %all-to-all-done.5 = f32[32,2,2,2,32,128]{5,4,3,2,1,0:T(8,128)} async-done(((f32[32,2,2,2,32,128]{5,4,3,2,1,0:T(8,128)}), f32[32,2,2,2,32,128]{5,4,3,2,1,0:T(8,128)}, u32[]{:S(2)}, u32[]{:S(2)}) %all-to-all-start.5) | async-done | bytes 4194336 | tf_op jit(solution)/shard_map/all_to_all | solution.py:107
  762.2 5.0 slice.308
  768.0 5.0 slice.258
  773.0 6.9 fusion.11
  779.9 9.0 %copy.175 = f32[2,2,64,128,32]{2,1,4,3,0:T(2,128)} copy(f32[2,2,64,128,32]{3,4,0,1,2:T(8,128)} %fusion.11) | data formatting | bytes 8388608 | tf_op jit(solution)/shard_map/transpose | solution.py:303
  788.9 8.8 %reshape.926 = f32[2,128,4096]{1,2,0:T(8,128)} reshape(f32[2,2,64,128,32]{2,1,4,3,0:T(2,128)} %copy.175) | data formatting | bytes 8388608 | tf_op jit(solution)/shard_map/reshape | solution.py:303
  797.7 5.7 copy.181
  805.1 14.5 %all_to_all.36 = f32[32,2,128,8]{2,3,1,0:T(8,128)S(1)} all-to-all(f32[32,2,128,8]{2,3,1,0:T(8,128)S(1)} %copy.179), channel_id=1, replica_groups=mesh['gx'=8,'gy'=4] {'gx','gy'}, dimensions={0} | all-to-all | bytes 524288 | tf_op jit(solution)/shard_map/all_to_all | solution.py:107
  (311 shorter events, 108.1 us)
Async XLA Ops:
  14.7 283.0 %copy-start.37 = (pred[64,2,32]{2,1,0:T(4,128)(4,1)}, pred[64,2,32]{2,1,0:T(4,128)(4,1)S(1)}, u32[]{:S(2)}) copy-start(pred[64,2,32]{2,1,0:T(4,128)(4,1)S(1)} %broadcast_and_fusion) | copy-start | bytes 12292
  14.7 282.9 %copy-start.84 = (f32[2,64]{1,0:T(2,128)}, f32[2,64]{1,0:T(2,128)S(1)}, u32[]{:S(2)}) copy-start(f32[2,64]{1,0:T(2,128)S(1)} %broadcast_select_fusion) | copy-start | bytes 1540
  15.7 4.1 copy-start.3
  15.7 4.1 copy-start.6
  29.0 58.9 %copy-start.45 = (f32[32,2,32,2,1,1]{2,0,3,1,5,4:T(8,128)S(1)}, f32[32,2,32,2,1,1]{2,0,3,1,5,4:T(8,128)}, u32[]{:S(2)}) copy-start(f32[32,2,32,2,1,1]{2,0,3,1,5,4:T(8,128)} %constant.184) | copy-start | bytes 49156
  29.0 58.9 %all-to-all-start = ((f32[32,2,2,34,128]{4,2,3,1,0:T(2,128)}), f32[32,2,2,34,128]{4,2,3,1,0:T(2,128)S(1)}, u32[]{:S(2)}, u32[]{:S(2)}) async-start(f32[32,2,2,34,128]{4,2,3,1,0:T(2,128)} %copy.122), calls=%async_computation | async-start | bytes 4456448 | tf_op jit(solution)/shard_map/all_to_all | solution.py:107
  37.0 65.9 %copy-start.88 = (s32[128]{0:T(128)}, s32[128]{0:T(128)S(1)}, u32[]{:S(2)}) copy-start(s32[128]{0:T(128)S(1)} %iota_multiply_fusion.1) | copy-start | bytes 1540
  37.0 50.9 %copy-start.94 = (pred[2]{0:T(512)(128)(4,1)}, pred[2]{0:T(512)(128)(4,1)S(1)}, u32[]{:S(2)}) copy-start(pred[2]{0:T(512)(128)(4,1)S(1)} %broadcast_compare_fusion) | copy-start | bytes 10
  37.1 66.4 %copy-start.82 = (s32[2,32]{1,0:T(2,128)}, s32[2,32]{1,0:T(2,128)S(1)}, u32[]{:S(2)}) copy-start(s32[2,32]{1,0:T(2,128)S(1)} %add_multiply_fusion.3) | copy-start | bytes 772
  37.8 65.7 %copy-start.86 = (pred[2,32]{1,0:T(4,128)(4,1)}, pred[2,32]{1,0:T(4,128)(4,1)S(1)}, u32[]{:S(2)}) copy-start(pred[2,32]{1,0:T(4,128)(4,1)S(1)} %get-tuple-element.131) | copy-start | bytes 196
  102.8 2.5 copy-start.60
  102.8 2.6 copy-start.62
  106.4 5.9 copy-start.70
  128.8 4.4 copy-start.68
  128.8 144.2 %all-to-all-start.1 = ((f32[32,2,2,96,128]{4,2,3,1,0:T(2,128)}), f32[32,2,2,96,128]{4,2,3,1,0:T(2,128)}, u32[]{:S(2)}, u32[]{:S(2)}) async-start(f32[32,2,2,96,128]{4,2,3,1,0:T(2,128)} %copy.139), calls=%async_computation.1 | async-start | bytes 12582912 | tf_op jit(solution)/shard_map/all_to_all | solution.py:107
  134.4 2.8 copy-start
  134.4 3.1 copy-start.14
  137.6 3.6 copy-start.32
  276.4 6.8 copy-start.23
  276.4 10.5 %copy-start.19 = (f32[32,2,2,32,128]{4,2,3,1,0:T(2,128)}, f32[32,2,2,32,128]{4,2,3,1,0:T(2,128)S(1)}, u32[]{:S(2)}) copy-start(f32[32,2,2,32,128]{4,2,3,1,0:T(2,128)S(1)} %get-tuple-element.34) | copy-start | bytes 6291460
  276.4 21.0 %copy-start.21 = (f32[32,2,2,32,128]{4,2,3,1,0:T(2,128)}, f32[32,2,2,32,128]{4,2,3,1,0:T(2,128)S(1)}, u32[]{:S(2)}) copy-start(f32[32,2,2,32,128]{4,2,3,1,0:T(2,128)S(1)} %get-tuple-element.35) | copy-start | bytes 6291460
  276.4 3.2 copy-start.1
  286.9 2.2 copy-start.11
  301.8 3.7 copy-start.31
  305.5 2.2 copy-start.4
  305.5 2.2 copy-start.7
  314.0 37.8 %all-to-all-start.2 = ((f32[32,2,2,22,128]{4,2,3,1,0:T(2,128)}), f32[32,2,2,22,128]{4,2,3,1,0:T(2,128)S(1)}, u32[]{:S(2)}, u32[]{:S(2)}) async-start(f32[32,2,2,22,128]{4,2,3,1,0:T(2,128)} %copy.150), calls=%async_computation.2 | async-start | bytes 2883584 | tf_op jit(solution)/shard_map/all_to_all | solution.py:107
  361.3 3.0 copy-start.71
  545.7 2.1 copy-start.15
  549.4 3.6 copy-start.33
  557.2 2.2 copy-start.12
  557.2 2.2 copy-start.85
  563.9 3.9 copy-start.22
  581.9 3.7 copy-start.41
  585.6 2.2 copy-start.8
  594.3 3.7 copy-start.77
  594.3 3.8 copy-start.78
  594.3 38.6 %copy-start.46 = (f32[32,2,32,2,1,1]{2,0,3,1,5,4:T(8,128)S(1)}, f32[32,2,32,2,1,1]{2,0,3,1,5,4:T(8,128)}, u32[]{:S(2)}) copy-start(f32[32,2,32,2,1,1]{2,0,3,1,5,4:T(8,128)} %constant.184) | copy-start | bytes 49156
  594.3 38.5 %all-to-all-start.4 = ((f32[32,2,2,22,128]{4,2,3,1,0:T(2,128)}), f32[32,2,2,22,128]{4,2,3,1,0:T(2,128)S(1)}, u32[]{:S(2)}, u32[]{:S(2)}) async-start(f32[32,2,2,22,128]{4,2,3,1,0:T(2,128)} %copy.167), calls=%async_computation.4 | async-start | bytes 2883584 | tf_op jit(solution)/shard_map/all_to_all | solution.py:107
  598.0 35.7 %copy-start.51 = (f32[32,128]{1,0:T(8,128)S(1)}, f32[32,128]{1,0:T(8,128)}, u32[]{:S(2)}) copy-start(f32[32,128]{1,0:T(8,128)} %constant.180) | copy-start | bytes 49156
  598.0 35.7 %copy-start.67 = (f32[32,128]{1,0:T(8,128)S(1)}, f32[32,128]{1,0:T(8,128)}, u32[]{:S(2)}) copy-start(f32[32,128]{1,0:T(8,128)} %constant.181) | copy-start | bytes 49156
  635.7 2.0 copy-start.30
  646.6 2.0 copy-start.96
  648.6 2.7 copy-start.69
  654.4 3.2 copy-start.76
  664.5 97.7 %all-to-all-start.5 = ((f32[32,2,2,2,32,128]{5,4,3,2,1,0:T(8,128)}), f32[32,2,2,2,32,128]{5,4,3,2,1,0:T(8,128)}, u32[]{:S(2)}, u32[]{:S(2)}) async-start(f32[32,2,2,2,32,128]{5,4,3,2,1,0:T(8,128)} %bitcast.503), calls=%async_computation.5 | async-start | bytes 8388608 | tf_op jit(solution)/shard_map/all_to_all | solution.py:107
  797.7 6.7 copy-start.42
  803.4 16.2 %copy-start.48 = (f32[2,256,256]{2,1,0:T(8,128)S(1)}, f32[2,256,256]{2,1,0:T(8,128)}, u32[]{:S(2)}) copy-start(f32[2,256,256]{2,1,0:T(8,128)} %constant.163.clone) | copy-start | bytes 1572868
  (54 other events, 80.5 us)
where the time goes:
time: 832 us; the launch traced here: 821 us
  waiting for transfers between devices  325 us (39%)
  blocking collectives  174 us (21%)
  matrix products  131 us (16%)
  local copies, waits for them, and re-layouts  114 us (14%)
  other arithmetic  45.1 us (5%)
  starting transfers between devices  22.3 us (3%)
  between operations  10.5 us (1%)
    all_to_all x5, waiting for transfers between devices, exchange(): return lax.all_to_all(values, AXES, split_axis=0, concat_axis=0, tiled=True)  325 us
    all_to_all x2, blocking collectives, exchange(): return lax.all_to_all(values, AXES, split_axis=0, concat_axis=0, tiled=True)  174 us
    dot_general x36, matrix products, contract(): jnp.einsum(pattern, left_side, right_side, precision=lax.Precision.HIGH)  128 us
    unnamed x209, local copies, waits for them, and re-layouts  33.5 us
    all_to_all x5, starting transfers between devices, exchange(): return lax.all_to_all(values, AXES, split_axis=0, concat_axis=0, tiled=True)  22.3 us
    transpose x3, local copies, waits for them, and re-layouts, contract(): jnp.einsum(pattern, left_side, right_side, precision=lax.Precision.HIGH)  19 us
  transfers between devices with their start and end apart: 5, of which 5 were waited for; matrix products, arithmetic and copies ran while one was open for 3% of the time, Pallas kernels for 0%

commit v1 on v0

v1 whole, which is shorter than its diff:
```python
import functools
import math

import jax
import jax.numpy as jnp
import numpy as np
from jax import lax
from jax.experimental import pallas as pl
from jax.experimental.pallas import tpu as pltpu
from jax.sharding import PartitionSpec as P

LOW = 256
SHELLS = 4
AXES = ("gx", "gy")

time_step = 0.05
viscosity = 0.05
coarse_ratio = 4.0


def contract(pattern, left_side, right_side):
    return jnp.einsum(pattern, left_side, right_side, precision=lax.Precision.HIGH)


def turn(product, length_of):
    phases = 2.0 * np.pi / length_of * (product % length_of)
    return np.cos(phases), np.sin(phases)


def rotation(cos_part, sin_part, axes):
    pairs = np.stack([np.stack([cos_part, -sin_part]), np.stack([sin_part, cos_part])])
    return np.moveaxis(pairs, (0, 1), axes).astype(np.float32)


def wave_tables(grid, total, rows):
    own = total // 2
    scale = 1.0 / math.sqrt(grid)
    t, a = np.arange(rows), np.arange(rows)
    b, D = np.arange(total), np.arange(total)
    out = {}
    cos_t, sin_t = turn(t[:, None] * a[None, :], rows)
    out["y1"] = np.stack([cos_t, -sin_t], 1).astype(np.float32)
    out["iy1"] = np.moveaxis(np.stack([cos_t, -sin_t], 1), 2, 0).astype(np.float32)
    ky = rows * D[None, :, None] + t[:, None, None]
    cos_t, sin_t = turn(ky * b[None, None, :], grid)
    sign = 1.0 - 2.0 * (b % 2)
    table = np.moveaxis(rotation(cos_t * scale, -sin_t * scale, (0, 1)), (0, 1), (2, 3))
    out["y2_low"] = table.copy()
    table[0, 0, 1] = np.stack([sign * scale, 0 * sign])
    table[0, own, 1] = np.stack([0 * sign + scale, 0 * sign])
    out["y2"] = table
    cos_t, sin_t = np.moveaxis(cos_t[:, :own], 1, 2), np.moveaxis(sin_t[:, :own], 1, 2)
    weight = np.where(ky[:, None, :own, 0] == 0, scale, 2.0 * scale)
    back = np.moveaxis(rotation(cos_t * weight, sin_t * weight, (0, 1)), (0, 1), (1, 4))
    back[0, :, :, 0, 1] = np.stack([sign * scale, 0 * sign])
    out["iy"] = back
    slope = np.moveaxis(rotation(-sin_t * weight, cos_t * weight, (0, 1)), (0, 1), (1, 4))
    slope[0, :, :, 0, :] = 0.0
    out["iyd"] = slope
    p, s = np.arange(total), np.arange(total)
    q, lane = np.arange(rows), np.arange(rows)
    cos_t, sin_t = turn(p[:, None] * s[None, :], total)
    out["x1"] = rotation(cos_t * scale, -sin_t * scale, (1, 3))
    cos_t, sin_t = turn(s[:own, None] * p[None, :], total)
    out["ix1"] = rotation(cos_t * scale, sin_t * scale, (1, 3))
    cos_t, sin_t = turn(q[:, None] * lane[None, :], rows)
    out["x2"] = rotation(cos_t.T, -sin_t.T, (2, 0))
    out["ix2"] = rotation(cos_t, sin_t, (2, 0))
    cos_t, sin_t = turn(p[:, None] * lane[None, :], grid)
    out["tw"] = np.stack([cos_t, sin_t]).astype(np.float32)
    return out


TILE = 16
PART = 32


def plus(one, two, sign=1.0):
    if two is None:
        return one
    if one is None:
        return tuple(sign * part for part in two)
    if sign > 0:
        return one[0] + two[0], one[1] + two[1]
    return one[0] - two[0], one[1] - two[1]


def turned_by(value, step, length, sign):
    if value is None:
        return None
    step = step % length
    real, imag = value
    if step == 0:
        return value
    if 2 * step == length:
        return -real, -imag
    if 4 * step == length:
        return (-imag, real) if sign > 0 else (imag, -real)
    if 4 * step == 3 * length:
        return (imag, -real) if sign > 0 else (-imag, real)
    angle = 2.0 * math.pi * step / length
    c, s = math.cos(angle), sign * math.sin(angle)
    return real * c - imag * s, real * s + imag * c


def small_fft(values, sign):
    size = len(values)
    if size == 1:
        return values
    even, odd = small_fft(values[::2], sign), small_fft(values[1::2], sign)
    odd = [turned_by(value, k, size, sign) for k, value in enumerate(odd)]
    return [plus(e, o) for e, o in zip(even, odd)] + [plus(e, o, -1.0) for e, o in zip(even, odd)]


def long_fft(total, load, store, between, sign, side=None):
    wide = 4
    deep = total // wide
    for j in range(deep):
        out = small_fft([load(deep * i + j) for i in range(wide)], sign)
        for u in range(wide):
            real, imag = turned_by(out[u], j * u, total, sign)
            between[u * deep + j, 0] = real
            between[u * deep + j, 1] = imag
    for u in range(wide):
        values = [(between[u * deep + j, 0], between[u * deep + j, 1]) for j in range(deep)]
        if side is None:
            for v, value in enumerate(small_fft(values, sign)):
                store(u + wide * v, value)
        else:
            even, odd = small_fft(values[::2], sign), small_fft(values[1::2], sign)
            for v in range(deep // 2):
                o = turned_by(odd[v], v, deep, sign)
                store(u + wide * v, (even[v][0] + side * o[0], even[v][1] + side * o[1]))


def split(value):
    high = value.astype(jnp.bfloat16)
    return high, (value - high.astype(jnp.float32)).astype(jnp.bfloat16)


def halves_of(table):
    table = np.asarray(table, np.float32)
    high = table.astype(jnp.bfloat16)
    return high, (table - high.astype(np.float32)).astype(jnp.bfloat16)


def dot3(left, right):
    def dot(a, b):
        return jnp.dot(a, b, preferred_element_type=jnp.float32)

    return dot(left[0], right[0]) + dot(left[1], right[0]) + dot(left[0], right[1])


def y_tables(grid, total, rows):
    scale = 1.0 / math.sqrt(grid)
    b, t, a = np.arange(total)[:, None, None], np.arange(rows)[None, :, None], np.arange(rows)
    cos_t, sin_t = turn(t * a * total + t * b, grid)
    forth = np.concatenate([cos_t, -sin_t], 1) * scale
    return forth, 2.0 * forth.transpose(0, 2, 1)


def x_tables(grid, total, rows):
    scale = 1.0 / math.sqrt(grid)
    l, q = np.arange(rows)[:, None], np.arange(rows)[None, :]
    cos_t, sin_t = turn(l * q, rows)
    forth = np.block([[cos_t, -sin_t], [sin_t, cos_t]]) * scale
    back = np.block([[cos_t, sin_t], [-sin_t, cos_t]]) * scale
    cos_t, sin_t = turn(np.arange(total)[:, None] * np.arange(rows)[None, :], grid)
    return forth, back, np.stack([cos_t, sin_t], 1).astype(np.float32)[:, :, None, :]


def params():
    return pltpu.CompilerParams(vmem_limit_bytes=56 * 1024 * 1024)


def forward_rows(total, rows, waves, out_ref, between):
    def tile(i, carry):
        spot = pl.ds(pl.multiple_of(i * TILE, TILE), TILE)
        low = pl.ds(pl.multiple_of(rows + i * TILE, TILE), TILE)

        def store(D, value):
            out_ref[D, 0, spot, :] = value[0]
            out_ref[D, 1, spot, :] = value[1]

        long_fft(total, lambda b: (waves[b, spot, :], waves[b, low, :]), store, between, -1.0)
        return carry

    lax.fori_loop(0, rows // TILE, tile, 0)
    top = pl.ds(0, 8)
    here = lax.broadcasted_iota(jnp.int32, (8, rows), 0) == 0
    middle = total // 2
    zero, other = out_ref[0, 0, top, :], out_ref[middle, 0, top, :]
    out_ref[0, 1, top, :] = jnp.where(here, other, out_ref[0, 1, top, :])
    out_ref[middle, 1, top, :] = jnp.where(here, zero, out_ref[middle, 1, top, :])


def start_kernel(total, rows, field, forth_hi, forth_lo, out_ref, waves, between):
    def step(b, carry):
        waves[b] = dot3((forth_hi[b], forth_lo[b]), split(field[b]))
        return carry

    lax.fori_loop(0, total, step, 0)
    forward_rows(total, rows, waves, out_ref, between)


def product_kernel(total, rows, unit, info, forth_hi, forth_lo, back_hi, back_lo, *refs):
    fields, out_ref, waves, left, right, between = refs[0], *refs[-5:]
    psi, psi_x, vort_x = (fields.at[:, i] for i in range(3))
    vort = fields.at[:, 3] if len(refs) == 6 else refs[1]
    own = total // 2
    offset = info[3]

    def waves_of(field, slope, begin):
        def tile(i, carry):
            spot = pl.ds(pl.multiple_of(i * TILE, TILE), TILE)
            top = pl.ds(pl.multiple_of(begin + i * TILE, TILE), TILE)
            low = pl.ds(pl.multiple_of(begin + rows + i * TILE, TILE), TILE)
            row = lax.broadcasted_iota(jnp.int32, (TILE, rows), 0) + (i * TILE + begin)
            here = row == 0

            def load(r):
                if r > own or (r == own and slope):
                    return None
                if r == own:
                    imag = field[0, 1, spot, :]
                    return jnp.where(here, 0.5 * imag, 0.0), jnp.zeros_like(imag)
                real, imag = field[r, 0, spot, :], field[r, 1, spot, :]
                if slope:
                    factor = (row + (r * rows - offset)).astype(jnp.float32) * unit
                    if r == 0:
                        factor = jnp.where(here, 0.0, factor)
                    return -factor * imag, factor * real
                if r == 0:
                    real = jnp.where(here, 0.5 * real, real)
                    imag = jnp.where(here, 0.0, imag)
                return real, imag

            def store(b, value):
                waves[b, top, :] = value[0]
                waves[b, low, :] = value[1]

            long_fft(total, load, store, between, 1.0)
            return carry

        lax.fori_loop(0, rows // TILE, tile, 0)

    def physical(b):
        return dot3((back_hi[b], back_lo[b]), split(waves[b]))

    def each(step):
        def run(b, carry):
            step(b)
            return carry

        lax.fori_loop(0, total, run, 0)

    def first(b):
        left[b] = physical(b)

    def second(b):
        left[b] = left[b] * physical(b)

    def third(b):
        right[b] = physical(b)

    def fourth(b):
        advect = left[b] - right[b] * physical(b)
        waves[b] = dot3((forth_hi[b], forth_lo[b]), split(advect))

    for field, slope, step in (
        (psi, True, first), (vort_x, False, second), (psi_x, False, third), (vort, True, fourth),
    ):
        waves_of(field, slope, 0)
        each(step)
    forward_rows(total, rows, waves, out_ref, between)


def spectral_kernel(total, rows, grid, stage, *refs):
    refs = list(refs)

    def take(count):
        out = refs[:count]
        del refs[:count]
        return out

    info, side_of, source, twist, forth_hi, forth_lo, back_hi, back_lo = take(8)
    state_in = take(1)[0] if stage > 0 else None
    moved_in, first_in = take(2) if stage == 2 else (None, None)
    drive_in = take(1)[0] if stage > 0 else None
    state_out = take(1)[0] if stage == 0 else None
    moved_out, first_out = take(2) if stage == 1 else (None, None)
    ahead_out, now_out = take(2) if stage == 2 else (None, None)
    counted = 3 + stage if stage < 2 else 0
    landed = take(1)[0] if counted else None
    ins, outs, between, kept, arrived, sent_sem, come_sem, own_sem = take(8)
    room, field_sent, field_come, field_own = take(4) if counted else [None] * 4
    extra_first = True
    unit = 2.0 * math.pi / grid
    step = pl.program_id(0)
    riding = step == 0
    width = lax.axis_size("gy")
    me = lax.axis_index("gx") * width + lax.axis_index("gy")
    own = total // 2
    base = (me // own) * own
    slot = me - base
    reach = total if stage == 0 else (grid // 3) // rows
    parts = rows // PART

    def near(device):
        return (device <= reach) | (device >= total - 1 - reach)

    def place(device):
        return (device // width, device % width)

    def move(part, k, extent):
        dest = (me + k) % total
        spot = pl.ds(pl.multiple_of(part * PART, PART), extent)
        return pltpu.make_async_remote_copy(
            src_ref=source.at[dest, :, spot, :],
            dst_ref=arrived.at[me, :, spot, :],
            send_sem=sent_sem.at[part, k],
            recv_sem=come_sem.at[part],
            device_id=place(dest),
            device_id_type=pl.DeviceIdType.MESH,
        )

    def all_moves(act):
        def run(n, carry):
            part, k = n // (total - 1), n % (total - 1) + 1
            dest = (me + k) % total

            @pl.when(near(dest))
            def _():
                act(move(part, k, PART))

            if reach < own:

                @pl.when((dest == own) & (part == 0))
                def _():
                    act(move(part, k, TILE))

            return carry

        lax.fori_loop(0, parts * (total - 1), run, 0)

    mine = pltpu.make_async_copy(source.at[me], arrived.at[me], own_sem.at[0])

    def await_part(part, extent):
        spot = pl.ds(pl.multiple_of(part * PART, PART), extent)
        ref = arrived.at[pl.ds(0, total - 1), :, spot, :]
        pltpu.make_async_copy(ref, ref, come_sem.at[part]).wait()

    @pl.when(riding)
    def _():
        all_moves(lambda copy: copy.start())
        mine.start()
        mine.wait()

        if reach < own:

            @pl.when(me == own)
            def _():
                await_part(0, TILE)

    every = PART // TILE

    @pl.when(near(me) & (riding | ((step > 1) & ((step - 1) % every == 0))))
    def _():
        await_part(jnp.maximum(step - 1, 0) // every, PART)

    spot_in = pl.ds(pl.multiple_of(jnp.maximum(step - 1, 0) * TILE, TILE), TILE)
    origin = info[2] == 1
    tile = step - 1
    size = TILE
    shape = (size, rows)
    row = lax.broadcasted_iota(jnp.int32, shape, 0)
    first_here = (row == 0) & (tile == 0) & origin if extra_first else None
    side = side_of[0]

    def block(p):
        return pl.ds(pl.multiple_of(p * size, size), size)

    def load(s):
        real, imag = arrived[s, 0, spot_in, :], arrived[s, 1, spot_in, :]
        if extra_first:
            ride = jnp.where(row == 0, imag, 0.0)
            imag = jnp.where(riding | first_here, 0.0, imag)
            real = jnp.where(riding, ride, real)
        return real, imag

    def store(p, value):
        c, s = twist[p, 0], twist[p, 1]
        ins[p * size : (p + 1) * size, :rows] = value[0] * c + value[1] * s
        ins[p * size : (p + 1) * size, rows:] = value[1] * c - value[0] * s

    long_fft(total, load, store, between, -1.0)
    chunk = 8 * size

    def multiply(hi, lo):
        def run(i, carry):
            spot = pl.ds(pl.multiple_of(i * chunk, chunk), chunk)
            outs[spot, :] = dot3(split(ins[spot, :]), (hi[...], lo[...]))
            return carry

        lax.fori_loop(0, total * size // chunk, run, 0)

    multiply(forth_hi, forth_lo)
    wave_y = info[0] + tile * size + row
    if extra_first:
        wave_y = jnp.where(riding, info[1], wave_y)
    q = lax.broadcasted_iota(jnp.int32, shape, 1)
    cutoff = info[4]
    rows_kept = jnp.abs(wave_y) <= cutoff
    y_squared = wave_y * wave_y

    def waves_x(p):
        kx = p + total * q
        wave = jnp.where(kx < grid // 2, kx, kx - grid)
        slope = jnp.where(kx == grid // 2, 0, wave).astype(jnp.float32) * unit
        return wave, slope

    def squares_of(wave):
        squares = wave * wave + y_squared
        return squares, squares.astype(jnp.float32) * (unit * unit)

    def pair(ref, p):
        return ref[p, 0], ref[p, 1]

    def put(ref, p, value):
        ref[p, 0] = value[0]
        ref[p, 1] = value[1]

    step_size = time_step * viscosity

    def settle(p, carry):
        wave, _ = waves_x(p)
        squares, lap = squares_of(wave)
        found = outs[block(p), :rows], outs[block(p), rows:]
        if stage == 0:
            put(state_out, p, found)
            return carry
        mask = rows_kept & (jnp.abs(wave) <= cutoff)
        term = tuple(d - jnp.where(mask, part, 0.0) for d, part in zip(pair(drive_in, p), found))
        state = pair(state_in, p)
        if stage == 1:
            put(first_out, p, term)
            put(moved_out, p, tuple(s - step_size * lap * s + time_step * t for s, t in zip(state, term)))
            return carry
        low = LOW // 2
        inside = (wave >= -low) & (wave < low) & (wave_y >= -low) & (wave_y < low)
        moved, first = pair(moved_in, p), pair(first_in, p)
        for c in (0, 1):
            linear = viscosity * lap * (state[c] + moved[c])
            now = state[c] + 0.5 * time_step * (first[c] + term[c] - linear)
            ahead = now + coarse_ratio * (now - state[c])
            ahead_out[p, c] = ahead
            now_out[p, c] = jnp.where(inside, ahead, now)
        return carry

    lax.fori_loop(0, total, settle, 0)
    whole = state_out if stage == 0 else moved_out

    for index in range(counted):

        def fill(p, carry):
            wave, slope = waves_x(p)
            real, imag = pair(whole, p)
            if index < 2:
                squares, lap = squares_of(wave)
                inverse = jnp.where(squares == 0, 0.0, 1.0 / jnp.maximum(lap, unit * unit))
                real, imag = inverse * real, inverse * imag
            if index in (1, 2):
                real, imag = -slope * imag, slope * real
            ins[block(p), :rows] = real
            ins[block(p), rows:] = imag
            return carry

        lax.fori_loop(0, total, fill, 0)
        multiply(back_hi, back_lo)

        def load_back(p):
            real, imag = outs[p * size : (p + 1) * size, :rows], outs[p * size : (p + 1) * size, rows:]
            c, s = twist[p, 0], twist[p, 1]
            return real * c - imag * s, imag * c + real * s

        def store_back(s, value):
            real, imag = value
            if extra_first:
                imag = jnp.where(first_here, kept[index, s], imag)
                kept[index, s] = real
            room[s, index, 0, spot_in, :] = real
            room[s, index, 1, spot_in, :] = imag

        long_fft(total, load_back, store_back, between, 1.0, side)

    if counted:

        def field_move(i, k):
            spot = pl.ds(pl.multiple_of(i * TILE, TILE), TILE)
            to = (slot + k) % own
            return pltpu.make_async_remote_copy(
                src_ref=room.at[to, :, :, spot, :],
                dst_ref=landed.at[slot, :, :, spot, :],
                send_sem=field_sent.at[i],
                recv_sem=field_come.at[i],
                device_id=place(base + to),
                device_id_type=pl.DeviceIdType.MESH,
            )

        def field_mine(i):
            spot = pl.ds(pl.multiple_of(i * TILE, TILE), TILE)
            return pltpu.make_async_copy(
                room.at[slot, :, :, spot, :], landed.at[slot, :, :, spot, :], field_own.at[i]
            )

        @pl.when(step > 0)
        def _():
            def run(k, carry):
                field_move(tile, k).start()
                return carry

            lax.fori_loop(1, own, run, 0)
            field_mine(tile).start()

    @pl.when(step == pl.num_programs(0) - 1)
    def _():
        all_moves(lambda copy: copy.wait_send())
        if counted:

            def run(i, carry):
                spot = pl.ds(pl.multiple_of(i * TILE, TILE), TILE)
                gone = room.at[pl.ds(0, own - 1), :, :, spot, :]
                come = landed.at[pl.ds(0, own - 1), :, :, spot, :]
                pltpu.make_async_copy(gone, gone, field_sent.at[i]).wait()
                pltpu.make_async_copy(come, come, field_come.at[i]).wait()
                field_mine(i).wait()
                return carry

            lax.fori_loop(0, rows // TILE, run, 0)


def narrow_body(vorticity_grid, forcing_grid, cutoff, forcing_shells):
    rows, grid = vorticity_grid.shape
    total = lax.axis_size("gx") * lax.axis_size("gy")
    own = total // 2
    rank = lax.axis_index("gx") * lax.axis_size("gy") + lax.axis_index("gy")
    half, lane_rank = rank // own, rank % own
    halves = [list(range(own)), list(range(own, total))]
    tables = wave_tables(grid, total, rows)
    half_low = LOW // 2
    unit = 2.0 * math.pi / grid
    cuts = 2
    cut = rows // cuts

    def exchange(values, groups=None):
        return lax.all_to_all(
            values, AXES, split_axis=0, concat_axis=0, tiled=True, axis_index_groups=groups
        )

    first_row = jnp.where(half == 0, 0, grid // 2) + lane_rank * rows
    first_wave = rank * rows - jnp.where(half == 0, 0, grid)

    def forward_y(fields, table):
        first = contract("tda,abx->tdbx", tables["y1"], fields)
        return contract("tDcdb,tdbx->Dctx", table, first)

    slope_of = (
        rows * jnp.arange(own)[None, :] + jnp.arange(rows)[:, None] - half * (grid // 2)
    ).astype(jnp.float32) * unit
    slope_table = tables["iyd"] * slope_of[:, None, None, :, None]

    def inverse_y(waves, table):
        first = contract("tdbrc,rctx->tdbx", table, waves)
        return contract("atd,tdbx->abx", tables["iy1"], first)

    tw_cos = tables["tw"][0][:, None, :]
    tw_sin = tables["tw"][1][:, None, :]
    flip = jnp.where((half == 1) & (jnp.arange(total) % 2 == 1), -1.0, 1.0)[:, None, None]
    tw_cos_back, tw_sin_back = tw_cos * flip, tw_sin * flip

    def forward_x(waves):
        first = contract("pdsc,sctl->pdtl", tables["x1"], waves)
        real, imag = first[:, 0], first[:, 1]
        first = jnp.stack([real * tw_cos + imag * tw_sin, imag * tw_cos - real * tw_sin], 1)
        return contract("pctl,cldq->pdtq", first, tables["x2"])

    def inverse_x(waves):
        first = contract("pctq,cqdl->pdtl", waves, tables["ix2"])
        real, imag = first[:, 0], first[:, 1]
        first = jnp.stack(
            [real * tw_cos_back - imag * tw_sin_back, imag * tw_cos_back + real * tw_sin_back], 1
        )
        return contract("sdpc,pctl->sdtl", tables["ix1"], first)

    p_ids = jnp.arange(total, dtype=jnp.int32)[:, None, None]
    q_ids = jnp.arange(rows, dtype=jnp.int32)[None, None, :]
    kx_ids = p_ids + total * q_ids
    wave_x = jnp.where(kx_ids < grid // 2, kx_ids, kx_ids - grid)
    deriv_x = jnp.where(kx_ids == grid // 2, 0, wave_x).astype(jnp.float32) * unit
    origin = lane_rank == 0
    extra_wave = jnp.where(half == 0, -(grid // 2), 0) + jnp.zeros((1, 1, 1), jnp.int32)

    def wave_y_of(piece):
        return first_wave + cut * piece + jnp.arange(cut, dtype=jnp.int32)[None, :, None]

    def laplacian(rows_y):
        return (wave_x * wave_x + rows_y * rows_y).astype(jnp.float32) * (unit * unit)

    def inverse_laplacian(rows_y):
        squares = wave_x * wave_x + rows_y * rows_y
        lap = squares.astype(jnp.float32) * (unit * unit)
        return jnp.where(squares == 0, 0.0, 1.0 / jnp.maximum(lap, unit * unit))

    def dealias(rows_y):
        return (jnp.abs(wave_x) <= cutoff[0]) & (jnp.abs(rows_y) <= cutoff[0])

    def slope_x(pair):
        return (-deriv_x * pair[1], deriv_x * pair[0])

    def packed(main, extra, piece):
        real, imag = main
        if piece == 0:
            here = origin & (jnp.arange(cut) == 0)[None, :, None]
            real = jnp.where(here, real - extra[1], real)
            imag = jnp.where(here, imag + extra[0], imag)
        return jnp.stack([real, imag], 1)

    def spectra_of(sent):
        pieces, extra = [], None
        for piece in range(cuts):
            waves = exchange(sent[:, :, piece * cut : (piece + 1) * cut])
            if piece == 0:
                riding = waves[:, 1:, :1]
                extra = forward_x(jnp.concatenate([riding, jnp.zeros_like(riding)], 1))
                extra = (extra[:, 0], extra[:, 1])
                here = origin & (jnp.arange(cut) == 0)[:, None]
                clear = here & (jnp.arange(2) == 1)[:, None, None]
                waves = jnp.where(clear, 0.0, waves)
            out = forward_x(waves)
            pieces.append((out[:, 0], out[:, 1]))
        return pieces, extra

    def returned(pieces):
        return jnp.concatenate([exchange(inverse_x(part), halves) for part in pieces], 2)

    turned = vorticity_grid.T.reshape(rows, total, rows)
    start = forward_y(turned, tables["y2"])
    state, extra = spectra_of(start)

    share = half_low // total
    count_d = -(-half_low // rows)
    count_q = -(-half_low // total)
    force = forward_y(forcing_grid.T.reshape(rows, total, rows), tables["y2_low"][:, :count_d])
    force = force.transpose(0, 2, 1, 3).reshape(count_d * rows, 2, rows)[:half_low]
    force = exchange(force.reshape(total, share, 2, rows))
    force = forward_x(force.transpose(0, 2, 1, 3))
    force = jnp.concatenate([force[..., rows - count_q :], force[..., :count_q]], 3)
    force = force.transpose(2, 1, 3, 0).reshape(share, 2, LOW)
    force = lax.all_gather(force, AXES, axis=0, tiled=True)
    turned_force = jnp.roll(jnp.flip(force, 2), 1, 2) * jnp.array([1.0, -1.0])[None, :, None]
    turned_force = jnp.roll(jnp.flip(turned_force, 0), 1, 0)
    force_all = jnp.concatenate([turned_force, force], 0)

    def spread(part):
        part = part.reshape(part.shape[0], 2, 2 * count_q, total).transpose(1, 3, 0, 2)
        gap = jnp.zeros(part.shape[:3] + (rows - 2 * count_q,), jnp.float32)
        return jnp.concatenate([part[..., count_q:], gap, part[..., :count_q]], 3)

    def shell(rows_y):
        squares = wave_x * wave_x + rows_y * rows_y
        mask = jnp.zeros(squares.shape, bool)
        for index in range(SHELLS):
            radius = forcing_shells[index]
            mask = mask | ((radius * radius <= squares) & (squares < (radius + 1) * (radius + 1)))
        return mask

    def drive_of(piece):
        base = jnp.clip(first_wave + cut * piece + half_low, 0, LOW - cut)
        part = spread(lax.dynamic_slice_in_dim(force_all, base, cut, 0))
        mask = shell(wave_y_of(piece))
        return tuple(jnp.where(mask, part[c], 0.0) for c in (0, 1))

    drive = [drive_of(piece) for piece in range(cuts)]
    part = spread(force[:1])
    mask = shell(extra_wave)
    drive_extra = tuple(jnp.where(mask, part[c], 0.0) for c in (0, 1))

    waves_y = [wave_y_of(piece) for piece in range(cuts)]
    laps = [laplacian(rows_y) for rows_y in waves_y]
    inv_laps = [inverse_laplacian(rows_y) for rows_y in waves_y]
    masks = [dealias(rows_y) for rows_y in waves_y]
    lap_extra, inv_lap_extra = laplacian(extra_wave), inverse_laplacian(extra_wave)
    mask_extra = dealias(extra_wave)

    def fields_of(pieces, extra):
        psi_extra = tuple(inv_lap_extra * part for part in extra)
        psis = [tuple(inv * part for part in pair) for inv, pair in zip(inv_laps, pieces)]
        out = [
            [packed(psi, psi_extra, i) for i, psi in enumerate(psis)],
            [packed(slope_x(psi), slope_x(psi_extra), i) for i, psi in enumerate(psis)],
            [packed(slope_x(pair), slope_x(extra), i) for i, pair in enumerate(pieces)],
            [packed(pair, extra, i) for i, pair in enumerate(pieces)],
        ]
        return out

    def product(psi, psi_x, vort_x, vort):
        advect = inverse_y(psi, slope_table) * inverse_y(vort_x, tables["iy"])
        advect = advect - inverse_y(psi_x, tables["iy"]) * inverse_y(vort, slope_table)
        pieces, extra = spectra_of(forward_y(advect, tables["y2"]))
        terms = [
            tuple(d - jnp.where(mask, part, 0.0) for d, part in zip(ds, pair))
            for ds, mask, pair in zip(drive, masks, pieces)
        ]
        extra = tuple(d - jnp.where(mask_extra, part, 0.0) for d, part in zip(drive_extra, extra))
        return terms, extra

    own_start = lax.dynamic_slice_in_dim(start, half * own, own, 0)
    sent = fields_of(state, extra)[:3]
    first, first_extra = product(*[returned(part) for part in sent], own_start)

    def ahead_of(pair, lap, term):
        return tuple(
            part - time_step * viscosity * lap * part + time_step * add
            for part, add in zip(pair, term)
        )

    moved = [ahead_of(pair, lap, term) for pair, lap, term in zip(state, laps, first)]
    moved_extra = ahead_of(extra, lap_extra, first_extra)
    sent = fields_of(moved, moved_extra)
    second, _ = product(*[returned(part) for part in sent])

    def stepped(part, ahead, lap, one, two):
        return part + 0.5 * time_step * (one + two - viscosity * lap * (part + ahead))

    low_x = (wave_x >= -half_low) & (wave_x < half_low)
    outs, lows = [], []
    for i in range(cuts):
        low = low_x & (waves_y[i] >= -half_low) & (waves_y[i] < half_low)
        parts, low_parts = [], []
        for c in (0, 1):
            now = stepped(state[i][c], moved[i][c], laps[i], first[i][c], second[i][c])
            ahead = now + coarse_ratio * (now - state[i][c])
            parts.append(jnp.where(low, ahead, now))
            low_parts.append(
                jnp.concatenate([ahead[..., rows - count_q :], ahead[..., :count_q]], -1)
            )
        outs.append(jnp.stack(parts))
        lows.append(jnp.stack(low_parts))
    block = jnp.concatenate(lows, 2)
    spectrum = jnp.concatenate(outs, 2).transpose(0, 2, 3, 1).reshape(2, rows, grid)

    part_of = LOW // total
    signed = np.arange(LOW) - half_low
    spots = np.arange(LOW)
    col_cos, col_sin = (
        t.astype(np.float32) / 16.0 for t in turn(signed[:, None] * spots[None, :], LOW)
    )
    column = np.stack([np.stack([col_cos, col_sin]), np.stack([-col_sin, col_cos])])
    column = column.reshape(2, 2, 2 * count_q, total, LOW)
    mixed = contract("cptq,cdqpa->dta", block, column)
    mixed = mixed.reshape(2, rows, total, part_of).transpose(2, 0, 1, 3)
    mixed = exchange(mixed)
    mixed = jnp.concatenate([mixed[total - count_d :], mixed[:count_d]], 0)
    mixed = mixed.transpose(1, 0, 2, 3).reshape(2, 2 * count_d * rows, part_of)
    if count_d * rows != half_low:
        mixed = mixed[:, count_d * rows - half_low : count_d * rows + half_low]
    coarse = contract("cqa,cqb->ab", mixed, np.stack([col_cos, -col_sin]))
    return (spectrum, coarse)


def transfer_kernel(total, jobs, *refs):
    count = len(jobs)
    sources, results = refs[:count], refs[count : 2 * count]
    sent, arrived, local = refs[2 * count :]
    width = lax.axis_size("gy")
    me = lax.axis_index("gx") * width + lax.axis_index("gy")
    own = total // 2

    def copies(action):
        for index, (size, begin, extent, reach, mode) in enumerate(jobs):
            source, result = sources[index], results[index]
            base = (me // size) * size
            slot = me - base

            def block(place, rows):
                if mode == "gather":
                    return source
                if extent is None:
                    return source.at[place]
                return source.at[place, :, pl.ds(begin, rows), :]

            def landing(place, rows):
                if extent is None or rows == extent:
                    return result.at[place]
                return result.at[place, :, pl.ds(0, rows), :]

            def move(k, dest, rows):
                return pltpu.make_async_remote_copy(
                    src_ref=block(dest - base, rows),
                    dst_ref=landing(slot, rows),
                    send_sem=sent.at[index, k],
                    recv_sem=arrived.at[index, k],
                    device_id=(dest // width, dest % width),
                    device_id_type=pl.DeviceIdType.MESH,
                )

            def wanted(device):
                if reach is None:
                    return [(None, extent)]
                near = (device <= reach) | (device >= total - 1 - reach)
                out = [(near, extent)]
                if begin == 0:
                    out.append(((device == own) & (own > reach), TILE))
                return out

            def guarded(condition, run):
                if condition is None:
                    run()
                else:
                    pl.when(condition)(run)

            def one(k, carry):
                dest = base + (slot + k) % size
                if mode == "ends":
                    source_ok = (me < reach) | (me >= total - reach)
                    origin = (me - k + total) % total
                    origin_ok = (origin < reach) | (origin >= total - reach)
                    if action != "arrived":
                        guarded(source_ok, lambda: getattr(move(k, dest, extent), "start" if action == "start" else "wait_send")())
                    else:
                        guarded(origin_ok, lambda: move(k, dest, extent).wait_recv())
                    return carry
                for condition, rows in wanted(me if action == "arrived" else dest):
                    if action == "start":
                        guarded(condition, lambda: move(k, dest, rows).start())
                    elif action == "sent":
                        guarded(condition, lambda: move(k, dest, rows).wait_send())
                    else:
                        guarded(condition, lambda: move(k, dest, rows).wait_recv())
                return carry

            if action == "start":
                here = pltpu.make_async_copy(
                    block(slot, extent), landing(slot, extent), local.at[index]
                )
                here.start()
            lax.fori_loop(1, size, one, 0)
            if action == "arrived":
                pltpu.make_async_copy(
                    block(slot, extent), landing(slot, extent), local.at[index]
                ).wait()

    copies("start")
    copies("sent")
    copies("arrived")


def transfer(total, number, *jobs):
    shapes, plans = [], []
    for source, size, begin, extent, reach, mode in jobs:
        dims = source.shape
        if mode == "gather":
            dims = (size,) + dims
        elif extent is not None:
            dims = dims[:2] + (extent,) + dims[3:]
        shapes.append(jax.ShapeDtypeStruct(dims, source.dtype))
        plans.append((size, begin, extent, reach, mode))
    anywhere = pl.BlockSpec(memory_space=pl.ANY)
    widest = max(plan[0] for plan in plans)
    return pl.pallas_call(
        functools.partial(transfer_kernel, total, tuple(plans)),
        out_shape=shapes,
        in_specs=[anywhere] * len(plans),
        out_specs=[anywhere] * len(plans),
        scratch_shapes=[
            pltpu.SemaphoreType.DMA((len(plans), widest)),
            pltpu.SemaphoreType.DMA((len(plans), widest)),
            pltpu.SemaphoreType.DMA((len(plans),)),
        ],
        compiler_params=pltpu.CompilerParams(has_side_effects=True),
        name=f"transfer{number}",
    )(*[job[0] for job in jobs])


def low_table(grid):
    angles = np.arange(grid)[:, None] * np.arange(LOW // 2)[None, :]
    cos_t, sin_t = turn(angles, grid)
    return (np.concatenate([cos_t, -sin_t], 1) / grid).astype(np.float32)


def force_rows(waves, rank):
    total, _, _, rows = waves.shape
    kx = np.arange(LOW) - LOW // 2
    cos_l, sin_l = turn(np.arange(rows)[:, None] * kx[None, :], total * rows)
    cos_s, sin_s = turn(np.arange(total)[:, None] * kx[None, :], total)
    table = rotation(cos_l, -sin_l, (2, 0))
    waves = contract("scnl,cldk->sdnk", waves, table)
    real, imag = waves[:, 0], waves[:, 1]
    c, s = (t.astype(np.float32)[:, None, :] for t in (cos_s, sin_s))
    return jnp.stack([(real * c + imag * s).sum(0), (imag * c - real * s).sum(0)])


def body(vorticity_grid, forcing_grid, cutoff, forcing_shells):
    rows, grid = vorticity_grid.shape
    total = lax.axis_size("gx") * lax.axis_size("gy")
    own = total // 2
    rank = lax.axis_index("gx") * lax.axis_size("gy") + lax.axis_index("gy")
    half, lane_rank = rank // own, rank % own
    half_low = LOW // 2
    unit = 2.0 * math.pi / grid

    first_wave = rank * rows - half * grid
    extra_wave = -(1 - half) * (grid // 2)
    info = jnp.stack(
        [
            first_wave, extra_wave, (lane_rank == 0).astype(jnp.int32), half * (grid // 2),
            cutoff[0], rank,
        ]
    ).astype(jnp.int32)
    side = (1.0 - 2.0 * half.astype(jnp.float32)).reshape(1)
    y_forth, y_back = y_tables(grid, total, rows)
    x_forth, x_back, twist = x_tables(grid, total, rows)
    y_forth, y_back = halves_of(y_forth), halves_of(y_back)
    x_forth, x_back = halves_of(x_forth), halves_of(x_back)
    smem = pl.BlockSpec(memory_space=pltpu.SMEM)
    vmem = pl.BlockSpec(memory_space=pltpu.VMEM)
    f32 = jnp.float32

    def shape(*dims):
        return jax.ShapeDtypeStruct(dims, f32)

    def scratch(*dims):
        return pltpu.VMEM(dims, f32)

    between = scratch(total, 2, TILE, rows)
    waves_room = scratch(total, 2 * rows, rows)
    send_shape = shape(total, 2, rows, rows)

    turned = vorticity_grid.reshape(rows, rows, total).transpose(2, 1, 0)
    start = pl.pallas_call(
        functools.partial(start_kernel, total, rows),
        out_shape=send_shape,
        in_specs=[vmem] * 3,
        out_specs=vmem,
        scratch_shapes=[waves_room, between],
        compiler_params=params(),
        name="start",
    )(turned, *y_forth)

    def product(*flat):
        return pl.pallas_call(
            functools.partial(product_kernel, total, rows, unit),
            out_shape=send_shape,
            in_specs=[smem] + [vmem] * (4 + len(flat)),
            out_specs=vmem,
            scratch_shapes=[
                waves_room, scratch(total, rows, rows), scratch(total, rows, rows), between,
            ],
            compiler_params=params(),
            name="product",
        )(info, *y_forth, *y_back, *flat)

    def spectral(stage, source, *inputs):
        steps = rows // TILE + 1
        count = 3 + stage if stage < 2 else 0
        plain = pl.BlockSpec((total, 2, TILE, rows), lambda i: (0, 0, i, 0))
        main = pl.BlockSpec((total, 2, TILE, rows), lambda i: (0, 0, jnp.maximum(i - 1, 0), 0))
        anywhere = pl.BlockSpec(memory_space=pl.ANY)
        whole = shape(total, 2, rows + TILE, rows)
        fields = shape(own, count, 2, rows, rows)
        if stage < 2:
            outs, out_specs = [whole] * (1 + stage) + [fields], [plain] * (1 + stage) + [anywhere]
        else:
            outs, out_specs = [shape(total, 2, rows, rows)] * 2, [main] * 2
        tables = (twist, *x_forth, *x_back)
        rooms = [
            scratch(total * TILE, 2 * rows), scratch(total * TILE, 2 * rows), between,
            scratch(4, own, TILE, rows), scratch(total, 2, rows, rows),
            pltpu.SemaphoreType.DMA((rows // PART, total)),
            pltpu.SemaphoreType.DMA((rows // PART,)),
            pltpu.SemaphoreType.DMA((1,)),
        ]
        if count:
            rooms += [scratch(own, count, 2, rows, rows)]
            rooms += [pltpu.SemaphoreType.DMA((rows // TILE,))] * 3
        return pl.pallas_call(
            functools.partial(spectral_kernel, total, rows, grid, stage),
            grid=(steps,),
            out_shape=outs,
            in_specs=[smem, smem, anywhere] + [vmem] * len(tables) + [plain] * len(inputs),
            out_specs=out_specs,
            scratch_shapes=rooms,
            compiler_params=pltpu.CompilerParams(
                vmem_limit_bytes=56 * 1024 * 1024, has_side_effects=True
            ),
            name=f"spectral{stage}",
        )(info, side, source, *tables, *inputs)

    count_q = -(-half_low // total)
    share = half_low // total
    force = contract("xy,yn->nx", forcing_grid, low_table(grid))
    force = force.reshape(2, total, share, rows).transpose(1, 0, 2, 3)
    (force,) = transfer(total, 0, (force, total, 0, None, None, "all"))
    force = force_rows(force, rank)
    (force,) = transfer(total, 1, (force, total, 0, None, None, "gather"))
    force = force.transpose(0, 2, 1, 3).reshape(half_low, 2, LOW)
    turned_force = jnp.roll(jnp.flip(force, 2), 1, 2) * jnp.array([1.0, -1.0])[None, :, None]
    turned_force = jnp.roll(jnp.flip(turned_force, 0), 1, 0)
    force_all = jnp.concatenate([turned_force, force], 0)
    wave_kx = jnp.arange(LOW, dtype=jnp.int32)[None, None, :] - half_low

    def drive_rows(part, rows_y):
        squares = wave_kx * wave_kx + rows_y * rows_y
        mask = jnp.zeros(squares.shape, bool)
        for index in range(SHELLS):
            radius = forcing_shells[index]
            mask = mask | ((radius * radius <= squares) & (squares < (radius + 1) * (radius + 1)))
        return jnp.where(mask, part, 0.0)

    part = lax.dynamic_slice_in_dim(
        force_all, jnp.clip(first_wave + half_low, 0, LOW - rows), rows, 0
    )
    part = drive_rows(part, first_wave + jnp.arange(rows, dtype=jnp.int32)[:, None, None])
    extra = drive_rows(force[:1], extra_wave)
    extra = jnp.concatenate([extra, jnp.zeros((TILE - 1,) + extra.shape[1:], f32)], 0)
    part = jnp.concatenate([extra, part], 0)
    part = part.reshape(part.shape[0], 2, 2 * count_q, total).transpose(3, 1, 0, 2)
    gap = jnp.zeros(part.shape[:3] + (rows - 2 * count_q,), f32)
    drive = jnp.concatenate([part[..., count_q:], gap, part[..., :count_q]], 3)

    state, fields = spectral(0, start)
    own_start = lax.dynamic_slice_in_dim(start, half * own, own, 0)
    advect = product(fields, own_start)
    moved, first, fields = spectral(1, advect, state, drive)
    advect = product(fields)
    ahead, now = spectral(2, advect, state, moved, first, drive)
    block = jnp.concatenate([ahead[..., rows - count_q :], ahead[..., :count_q]], -1)
    spectrum = now.transpose(1, 2, 3, 0).reshape(2, rows, grid)

    part_of = LOW // total
    count_d = -(-half_low // rows)
    signed = np.arange(LOW) - half_low
    spots = np.arange(LOW)
    col_cos, col_sin = (
        t.astype(np.float32) / 16.0 for t in turn(signed[:, None] * spots[None, :], LOW)
    )
    column = np.stack([np.stack([col_cos, col_sin]), np.stack([-col_sin, col_cos])])
    column = column.reshape(2, 2, 2 * count_q, total, LOW)
    mixed = contract("pctq,cdqpa->adt", block, column).reshape(total, part_of, 2, rows)
    (mixed,) = transfer(total, 7, (mixed, total, 0, None, count_d, "ends"))
    mixed = jnp.concatenate([mixed[total - count_d :], mixed[:count_d]], 0)
    mixed = mixed.transpose(2, 0, 3, 1).reshape(2, 2 * count_d * rows, part_of)
    coarse = contract("cqa,cqb->ab", mixed, np.stack([col_cos, -col_sin]))
    return (spectrum, coarse)


def solution(mesh):
    placed = (P(AXES, None), P(AXES, None), P(), P())

    def run(vorticity_grid, *rest):
        rows = vorticity_grid.shape[0] // mesh.size
        chosen = body if rows % 128 == 0 and mesh.size >= 8 else narrow_body
        return jax.shard_map(
            chosen,
            mesh=mesh,
            in_specs=placed,
            out_specs=(P(None, AXES, None), P(AXES, None)),
            check_vma=False,
        )(vorticity_grid, *rest)

    return run
```

time: 832 us -> 636 us (0.76); the launches traced: 821 us -> 635 us
  Pallas kernels: 0 us -> 561 us
  waiting for transfers between devices: 325 us -> 0 us
  blocking collectives: 174 us -> 0 us
  matrix products: 131 us -> 10 us
  local copies, waits for them, and re-layouts: 114 us -> 48.9 us
  other arithmetic: 45.1 us -> 5.64 us
  starting transfers between devices: 22.3 us -> 0 us
    pallas_call x0 -> x9, Pallas kernels: none -> 561 us  [the longest x3 414 us: spectral(): pl.pallas_call(functools.partial(spectral_kernel, total, rows, grid, stag...]
    all_to_all x5 -> x0, waiting for transfers between devices: 325 us -> none  [exchange(): return lax.all_to_all(values, AXES, split_axis=0, concat_axis=0, tiled=True)]
    all_to_all x2 -> x0, blocking collectives: 174 us -> none  [exchange(): return lax.all_to_all(values, AXES, split_axis=0, concat_axis=0, tiled=True)]
    dot_general x36 -> x4, matrix products: 128 us -> 10 us  [contract(): jnp.einsum(pattern, left_side, right_side, precision=lax.Precision.HIGH)]
    unnamed x209 -> x18, local copies, waits for them, and re-layouts: 33.5 us -> 8.58 us
    all_to_all x5 -> x0, starting transfers between devices: 22.3 us -> none  [exchange(): return lax.all_to_all(values, AXES, split_axis=0, concat_axis=0, tiled=True)]
    transpose x3 -> x1, local copies, waits for them, and re-layouts: 19 us -> 0.83 us  [contract(): jnp.einsum(pattern, left_side, right_side, precision=lax.Precision.HIGH)]
    another operation x17 -> x1, other arithmetic: 12.2 us -> 0.6 us  [force_rows(): jnp.stack([(real * c + imag * s).sum(0), (imag * c - real * s).sum(0)])]
  transfers between devices with their start and end apart: 5 -> 0, of which waited for: 5 -> 0; matrix products, arithmetic and copies ran while one was open for 3% -> 0% of each run, Pallas kernels for 0% -> 0%
where the time goes in v1:
time: 636 us; the launch traced here: 635 us
  Pallas kernels  561 us (88%)
  local copies, waits for them, and re-layouts  48.9 us (8%)
  matrix products  10 us (2%)
  between operations  9.18 us (1%)
    pallas_call x3, Pallas kernels, spectral(): pl.pallas_call(functools.partial(spectral_kernel, total, rows, grid, stag...  414 us
    pallas_call x2, Pallas kernels, product(): pl.pallas_call(functools.partial(product_kernel, total, rows, unit), out_...  95.3 us
    pallas_call x3, Pallas kernels, transfer(): pl.pallas_call(functools.partial(transfer_kernel, total, tuple(plans)), o...  40.1 us

profile of v1, /device:TPU:0, one launch (start us, length us, event | category | flops | bytes accessed | tf_op | source)
XLA Modules:
  0.0 635.2 jit_solution(14282382646786728532)
XLA Ops:
  0.6 0.0 copy-start
  0.6 0.0 copy-start.3
  0.7 0.0 copy-start.4
  0.7 0.0 copy-start.5
  1.5 0.6 stack.36.refs_0_.info
  2.1 0.1 pad.8.clone
  2.2 0.1 pad.5.clone
  2.3 1.5 fusion.16
  11.2 0.2 fusion.8
  11.4 0.0 copy-start.6
  11.4 5.6 fusion.17
  17.0 0.7 copy.67
  17.7 15.4 %transfer0.1 = f32[32,2,4,128]{3,2,1,0:T(4,128)} custom-call(f32[32,2,4,128]{3,2,1,0:T(4,128)} %bitcast.91), custom_call_target="tpu_custom_call" | custom-call | tf_op jit(solution)/shard_map/transfer0/pallas_call | solution.py:870
  33.2 1.2 convolution_bitcast_fusion
  34.4 0.1 add_reduce_fusion
  34.4 0.6 pad_maximum_fusion.2.refs_0_
  35.0 11.1 %transfer1.1 = f32[32,2,4,256]{3,2,1,0:T(4,128)} custom-call(f32[2,4,256]{2,1,0:T(4,128)} %pad_maximum_fusion.2.refs_0_), custom_call_target="tpu_custom_call" | custom-call | tf_op jit(solution)/shard_map/transfer1/pallas_call | solution.py:870
  46.2 1.1 copy.44
  47.3 0.3 slice.90
  47.7 0.7 reverse.4
  48.3 0.3 slice.106
  48.7 0.3 maximum_multiply_fusion
  49.1 0.7 broadcast_select_fusion
  49.9 0.2 pad_maximum_fusion.1
  50.1 0.2 copy.45
  50.3 1.9 copy.39
  52.2 2.6 copy.66
  54.8 12.5 %start.1.refs_2_ = f32[32,2,128,128]{3,2,1,0:T(8,128)} custom-call(f32[32,128,128]{2,1,0:T(8,128)} %bitcast.78, bf16[32,256,128]{2,1,0:T(8,128)(2,1)} %constant.98.clone.forth_hi, bf16[32,256,128]{2,1,0:T(8,128)(2,1)} %constant.99.clone.forth_lo), custom_call_target="tpu_custom_call" | custom-call | tf_op jit(solution)/shard_map/start/pallas_call | solution.py:940
  67.3 3.2 constant_dynamic-slice_fusion.refs_1_
  70.5 2.9 copy.46
  73.4 5.5 fusion.13
  79.0 3.5 pad_maximum_fusion.refs_9_.refs_11_
  82.4 151.1 %spectral0.1 = (f32[32,2,144,128]{3,2,1,0:T(8,128)}, f32[16,3,2,128,128]{4,3,2,1,0:T(8,128)}) custom-call(s32[6]{0:T(128)} %stack.36.refs_0_.info, f32[1]{0:T(128)} %bitcast.5.refs_1_, f32[32,2,128,128]{3,2,1,0:T(8,128)} %start.1.refs_2_, f32[32,2,1,128]{3,2,1,0:T(1,128)} %constant.105.clone.refs_3_, bf16[256,256]{1,0:T(8,128)(2,1)} %constant.106.clone.refs_4_, ...), custom_call_target="tpu_custom_call" | custom-call | tf_op jit(solution)/shard_map/spectral0/pallas_call | solution.py:986
  233.5 47.6 %product.2.refs_2_ = f32[32,2,128,128]{3,2,1,0:T(8,128)} custom-call(s32[6]{0:T(128)} %stack.36.refs_0_.info, bf16[32,256,128]{2,1,0:T(8,128)(2,1)} %constant.98.clone.forth_hi, bf16[32,256,128]{2,1,0:T(8,128)(2,1)} %constant.99.clone.forth_lo, bf16[32,128,256]{2,1,0:T(8,128)(2,1)} %constant.110.clone.back_hi, ...), custom_call_target="tpu_custom_call" | custom-call | tf_op jit(solution)/shard_map/product/pallas_call | solution.py:951
  281.2 171.8 %spectral1.1 = (f32[32,2,144,128]{3,2,1,0:T(8,128)}, f32[32,2,144,128]{3,2,1,0:T(8,128)}, f32[16,4,2,128,128]{4,3,2,1,0:T(8,128)}) custom-call(s32[6]{0:T(128)} %stack.36.refs_0_.info, f32[1]{0:T(128)} %bitcast.5.refs_1_, f32[32,2,128,128]{3,2,1,0:T(8,128)} %product.2.refs_2_, f32[32,2,1,128]{3,2,1,0:T(1,128)} %constant.105.clone.refs_3_, ...), custom_call_target="tpu_custom_call" | custom-call | tf_op jit(solution)/shard_map/spectral1/pallas_call | solution.py:986
  453.0 47.6 %product.3.refs_2_ = f32[32,2,128,128]{3,2,1,0:T(8,128)} custom-call(s32[6]{0:T(128)} %stack.36.refs_0_.info, bf16[32,256,128]{2,1,0:T(8,128)(2,1)} %constant.98.clone.forth_hi, bf16[32,256,128]{2,1,0:T(8,128)(2,1)} %constant.99.clone.forth_lo, bf16[32,128,256]{2,1,0:T(8,128)(2,1)} %constant.110.clone.back_hi, ...), custom_call_target="tpu_custom_call" | custom-call | tf_op jit(solution)/shard_map/product/pallas_call | solution.py:951
  500.6 90.6 %spectral2.1 = (f32[32,2,128,128]{3,2,1,0:T(8,128)}, f32[32,2,128,128]{3,2,1,0:T(8,128)}) custom-call(s32[6]{0:T(128)} %stack.36.refs_0_.info, f32[1]{0:T(128)} %bitcast.5.refs_1_, f32[32,2,128,128]{3,2,1,0:T(8,128)} %product.3.refs_2_, f32[32,2,1,128]{3,2,1,0:T(1,128)} %constant.105.clone.refs_3_, bf16[256,256]{1,0:T(8,128)(2,1)} %constant.106.clone.refs_4_, ...), custom_call_target="tpu_custom_call" | custom-call | tf_op jit(solution)/shard_map/spectral2/pallas_call | solution.py:986
  591.2 5.5 copy.47
  596.7 5.6 copy.52
  602.3 8.0 %fusion.14 = (f32[32,2,128,4]{3,2,1,0:T(8,128)}, f32[32,2,128,4]{3,2,1,0:T(8,128)}) fusion(f32[32,2,128,128]{3,2,1,0:T(8,128)} %get-tuple-element.15), kind=kLoop, calls=%fused_computation.47 | loop fusion | bytes 524288 | tf_op jit(solution)/shard_map/slice | solution.py:1037
  610.3 3.0 copy.48
  613.3 3.5 copy.49
  616.8 1.4 convolution_bitcast_fusion.1
  618.2 0.8 copy.50
  619.0 13.5 %transfer7.1 = f32[32,8,2,128]{3,2,1,0:T(2,128)} custom-call(f32[32,8,2,128]{3,2,1,0:T(2,128)} %bitcast.87), custom_call_target="tpu_custom_call" | custom-call | tf_op jit(solution)/shard_map/transfer7/pallas_call | solution.py:870
  632.6 0.7 fusion.15
  633.3 1.9 convolution_bitcast_fusion.2
  635.2 0.0 copy-done.1
  (19 shorter events, 0.2 us)
Async XLA Ops:
  0.6 10.8 %copy-start = (f32[128,4096]{1,0:T(8,128)S(1)}, f32[128,4096]{1,0:T(8,128)}, u32[]{:S(2)}) copy-start(f32[128,4096]{1,0:T(8,128)} %param.21) | copy-start | bytes 6291460
  0.6 32.5 %copy-start.3 = (f32[2,128,2,256,1]{3,1,0,2,4:T(8,128)S(1)}, f32[2,128,2,256,1]{3,1,0,2,4:T(8,128)}, u32[]{:S(2)}) copy-start(f32[2,128,2,256,1]{3,1,0,2,4:T(8,128)} %constant.116) | copy-start | bytes 1572868
  0.7 33.7 %copy-start.4 = (f32[32,256]{1,0:T(8,128)S(1)}, f32[32,256]{1,0:T(8,128)}, u32[]{:S(2)}) copy-start(f32[32,256]{1,0:T(8,128)} %constant.115) | copy-start | bytes 98308
  0.7 33.7 %copy-start.5 = (f32[32,256]{1,0:T(8,128)S(1)}, f32[32,256]{1,0:T(8,128)}, u32[]{:S(2)}) copy-start(f32[32,256]{1,0:T(8,128)} %constant.114) | copy-start | bytes 98308
  11.4 37.3 %copy-start.6 = (f32[2]{0:T(128)S(1)}, f32[2]{0:T(128)}, u32[]{:S(2)}) copy-start(f32[2]{0:T(128)} %constant.104.clone) | copy-start | bytes 28
  610.3 6.5 %copy-start.2 = (f32[2,2,8,32,256]{4,2,0,1,3:T(8,128)S(1)}, f32[2,2,8,32,256]{4,2,0,1,3:T(8,128)}, u32[]{:S(2)}) copy-start(f32[2,2,8,32,256]{4,2,0,1,3:T(8,128)} %constant.112.clone) | copy-start | bytes 3145732
  610.3 24.8 %copy-start.1 = (f32[128,4096]{1,0:T(8,128)S(1)}, f32[128,4096]{1,0:T(8,128)}, u32[]{:S(2)}) copy-start(f32[128,4096]{1,0:T(8,128)} %param.21) | copy-start | bytes 6291460

commit v2 on v1

--- a/solution.py
+++ b/solution.py
@@ -73,6 +73,8 @@
 
 TILE = 16
 PART = 32
+GROUP = 4
+FLIGHT = 2
 
 
 def plus(one, two, sign=1.0):
@@ -144,11 +146,25 @@
     return high, (table - high.astype(np.float32)).astype(jnp.bfloat16)
 
 
-def dot3(left, right):
-    def dot(a, b):
-        return jnp.dot(a, b, preferred_element_type=jnp.float32)
-
-    return dot(left[0], right[0]) + dot(left[1], right[0]) + dot(left[0], right[1])
+def dot(left, right):
+    return jnp.dot(left, right, preferred_element_type=jnp.float32)
+
+
+def stacked(table):
+    return np.concatenate(halves_of(table), -2)
+
+
+def table_times(table, data):
+    rows, columns = table.shape[0] // 2, data.shape[1]
+    found = dot(table, jnp.concatenate(split(data), 1))
+    return found[:rows, :columns] + (found[:rows, columns:] + found[rows:, :columns])
+
+
+def times_table(data, high_table, low_table):
+    rows = data.shape[0]
+    high, low = split(data)
+    found = dot(jnp.concatenate([high, low], 0), high_table)
+    return found[:rows] + (found[rows:] + dot(high, low_table))
 
 
 def y_tables(grid, total, rows):
@@ -194,19 +210,23 @@
     out_ref[middle, 1, top, :] = jnp.where(here, zero, out_ref[middle, 1, top, :])
 
 
-def start_kernel(total, rows, field, forth_hi, forth_lo, out_ref, waves, between):
-    def step(b, carry):
-        waves[b] = dot3((forth_hi[b], forth_lo[b]), split(field[b]))
+def start_kernel(total, rows, field, forth, out_ref, waves, between):
+    def step(i, carry):
+        spots = [i * GROUP + j for j in range(GROUP)]
+        found = [table_times(forth[b], field[b]) for b in spots]
+        for b, value in zip(spots, found):
+            waves[b] = value
         return carry
 
-    lax.fori_loop(0, total, step, 0)
+    lax.fori_loop(0, total // GROUP, step, 0)
     forward_rows(total, rows, waves, out_ref, between)
 
 
-def product_kernel(total, rows, unit, info, forth_hi, forth_lo, back_hi, back_lo, *refs):
+def product_kernel(total, rows, unit, info, forth, back, *refs):
     fields, out_ref, waves, left, right, between = refs[0], *refs[-5:]
     psi, psi_x, vort_x = (fields.at[:, i] for i in range(3))
-    vort = fields.at[:, 3] if len(refs) == 6 else refs[1]
+    own = total // 2
+    vort = fields.at[:, 3] if len(refs) == 6 else refs[1].at[pl.ds(info[6], own)]
     own = total // 2
     offset = info[3]
 
@@ -244,28 +264,33 @@
 
         lax.fori_loop(0, rows // TILE, tile, 0)
 
-    def physical(b):
-        return dot3((back_hi[b], back_lo[b]), split(waves[b]))
+    def physical(spots):
+        return [table_times(back[b], waves[b]) for b in spots]
 
     def each(step):
-        def run(b, carry):
-            step(b)
+        def run(i, carry):
+            step([i * GROUP + j for j in range(GROUP)])
             return carry
 
-        lax.fori_loop(0, total, run, 0)
-
-    def first(b):
-        left[b] = physical(b)
-
-    def second(b):
-        left[b] = left[b] * physical(b)
-
-    def third(b):
-        right[b] = physical(b)
-
-    def fourth(b):
-        advect = left[b] - right[b] * physical(b)
-        waves[b] = dot3((forth_hi[b], forth_lo[b]), split(advect))
+        lax.fori_loop(0, total // GROUP, run, 0)
+
+    def put(ref, spots, values):
+        for b, value in zip(spots, values):
+            ref[b] = value
+
+    def first(spots):
+        put(left, spots, physical(spots))
+
+    def second(spots):
+        put(left, spots, [left[b] * value for b, value in zip(spots, physical(spots))])
+
+    def third(spots):
+        put(right, spots, physical(spots))
+
+    def fourth(spots):
+        values = physical(spots)
+        advect = [left[b] - right[b] * value for b, value in zip(spots, values)]
+        put(waves, spots, [table_times(forth[b], value) for b, value in zip(spots, advect)])
 
     for field, slope, step in (
         (psi, True, first), (vort_x, False, second), (psi_x, False, third), (vort, True, fourth),
@@ -312,8 +337,13 @@
     def place(device):
         return (device // width, device % width)
 
+    def partner(k):
+        return jnp.where(
+            k % 2 == 0, (own - base) + (slot + k // 2) % own, base + (slot + (k + 1) // 2) % own
+        )
+
     def move(part, k, extent):
-        dest = (me + k) % total
+        dest = partner(k)
         spot = pl.ds(pl.multiple_of(part * PART, PART), extent)
         return pltpu.make_async_remote_copy(
             src_ref=source.at[dest, :, spot, :],
@@ -324,10 +354,10 @@
             device_id_type=pl.DeviceIdType.MESH,
         )
 
-    def all_moves(act):
+    def all_moves(begin, end, act):
         def run(n, carry):
-            part, k = n // (total - 1), n % (total - 1) + 1
-            dest = (me + k) % total
+            part, k = n // (total - 1), n % (total - 1)
+            dest = partner(k)
 
             @pl.when(near(dest))
             def _():
@@ -341,7 +371,7 @@
 
             return carry
 
-        lax.fori_loop(0, parts * (total - 1), run, 0)
+        lax.fori_loop(begin * (total - 1), end * (total - 1), run, 0)
 
     mine = pltpu.make_async_copy(source.at[me], arrived.at[me], own_sem.at[0])
 
@@ -352,7 +382,7 @@
 
     @pl.when(riding)
     def _():
-        all_moves(lambda copy: copy.start())
+        all_moves(0, FLIGHT, lambda copy: copy.start())
         mine.start()
         mine.wait()
 
@@ -364,9 +394,16 @@
 
     every = PART // TILE
 
-    @pl.when(near(me) & (riding | ((step > 1) & ((step - 1) % every == 0))))
+    part_here = jnp.maximum(step - 1, 0) // every
+    fresh = riding | ((step > 1) & ((step - 1) % every == 0))
+
+    @pl.when(near(me) & fresh)
     def _():
-        await_part(jnp.maximum(step - 1, 0) // every, PART)
+        await_part(part_here, PART)
+
+    @pl.when(fresh & (part_here < parts - FLIGHT))
+    def _():
+        all_moves(part_here + FLIGHT, part_here + FLIGHT + 1, lambda copy: copy.start())
 
     spot_in = pl.ds(pl.multiple_of(jnp.maximum(step - 1, 0) * TILE, TILE), TILE)
     origin = info[2] == 1
@@ -378,7 +415,7 @@
     side = side_of[0]
 
     def block(p):
-        return pl.ds(pl.multiple_of(p * size, size), size)
+        return pl.ds(pl.multiple_of(p * GROUP * size, GROUP * size), GROUP * size)
 
     def load(s):
         real, imag = arrived[s, 0, spot_in, :], arrived[s, 1, spot_in, :]
@@ -394,12 +431,12 @@
         ins[p * size : (p + 1) * size, rows:] = value[1] * c - value[0] * s
 
     long_fft(total, load, store, between, -1.0)
-    chunk = 8 * size
+    chunk = 16 * size
 
     def multiply(hi, lo):
         def run(i, carry):
             spot = pl.ds(pl.multiple_of(i * chunk, chunk), chunk)
-            outs[spot, :] = dot3(split(ins[spot, :]), (hi[...], lo[...]))
+            outs[spot, :] = times_table(ins[spot, :], hi[...], lo[...])
             return carry
 
         lax.fori_loop(0, total * size // chunk, run, 0)
@@ -413,8 +450,12 @@
     rows_kept = jnp.abs(wave_y) <= cutoff
     y_squared = wave_y * wave_y
 
+    q = lax.broadcasted_iota(jnp.int32, (GROUP,) + shape, 2)
+    lead = lax.broadcasted_iota(jnp.int32, (GROUP,) + shape, 0)
+    wave_y, y_squared, rows_kept = wave_y[None], y_squared[None], rows_kept[None]
+
     def waves_x(p):
-        kx = p + total * q
+        kx = p * GROUP + lead + total * q
         wave = jnp.where(kx < grid // 2, kx, kx - grid)
         slope = jnp.where(kx == grid // 2, 0, wave).astype(jnp.float32) * unit
         return wave, slope
@@ -423,19 +464,24 @@
         squares = wave * wave + y_squared
         return squares, squares.astype(jnp.float32) * (unit * unit)
 
+    def spots(p):
+        return pl.ds(p * GROUP, GROUP)
+
     def pair(ref, p):
-        return ref[p, 0], ref[p, 1]
+        return ref[spots(p), 0], ref[spots(p), 1]
 
     def put(ref, p, value):
-        ref[p, 0] = value[0]
-        ref[p, 1] = value[1]
+        ref[spots(p), 0] = value[0]
+        ref[spots(p), 1] = value[1]
 
     step_size = time_step * viscosity
 
     def settle(p, carry):
         wave, _ = waves_x(p)
         squares, lap = squares_of(wave)
-        found = outs[block(p), :rows], outs[block(p), rows:]
+        found = tuple(
+            part.reshape(GROUP, size, rows) for part in (outs[block(p), :rows], outs[block(p), rows:])
+        )
         if stage == 0:
             put(state_out, p, found)
             return carry
@@ -453,11 +499,11 @@
             linear = viscosity * lap * (state[c] + moved[c])
             now = state[c] + 0.5 * time_step * (first[c] + term[c] - linear)
             ahead = now + coarse_ratio * (now - state[c])
-            ahead_out[p, c] = ahead
-            now_out[p, c] = jnp.where(inside, ahead, now)
+            ahead_out[spots(p), c] = pltpu.roll(ahead, LOW // 2 // total, 2)
+            now_out[spots(p), c] = jnp.where(inside, ahead, now)
         return carry
 
-    lax.fori_loop(0, total, settle, 0)
+    lax.fori_loop(0, total // GROUP, settle, 0)
     whole = state_out if stage == 0 else moved_out
 
     for index in range(counted):
@@ -471,11 +517,11 @@
                 real, imag = inverse * real, inverse * imag
             if index in (1, 2):
                 real, imag = -slope * imag, slope * real
-            ins[block(p), :rows] = real
-            ins[block(p), rows:] = imag
+            ins[block(p), :rows] = real.reshape(GROUP * size, rows)
+            ins[block(p), rows:] = imag.reshape(GROUP * size, rows)
             return carry
 
-        lax.fori_loop(0, total, fill, 0)
+        lax.fori_loop(0, total // GROUP, fill, 0)
         multiply(back_hi, back_lo)
 
         def load_back(p):
@@ -524,7 +570,7 @@
 
     @pl.when(step == pl.num_programs(0) - 1)
     def _():
-        all_moves(lambda copy: copy.wait_send())
+        all_moves(0, parts, lambda copy: copy.wait_send())
         if counted:
 
             def run(i, carry):
@@ -768,136 +814,20 @@
     return (spectrum, coarse)
 
 
-def transfer_kernel(total, jobs, *refs):
-    count = len(jobs)
-    sources, results = refs[:count], refs[count : 2 * count]
-    sent, arrived, local = refs[2 * count :]
-    width = lax.axis_size("gy")
-    me = lax.axis_index("gx") * width + lax.axis_index("gy")
-    own = total // 2
-
-    def copies(action):
-        for index, (size, begin, extent, reach, mode) in enumerate(jobs):
-            source, result = sources[index], results[index]
-            base = (me // size) * size
-            slot = me - base
-
-            def block(place, rows):
-                if mode == "gather":
-                    return source
-                if extent is None:
-                    return source.at[place]
-                return source.at[place, :, pl.ds(begin, rows), :]
-
-            def landing(place, rows):
-                if extent is None or rows == extent:
-                    return result.at[place]
-                return result.at[place, :, pl.ds(0, rows), :]
-
-            def move(k, dest, rows):
-                return pltpu.make_async_remote_copy(
-                    src_ref=block(dest - base, rows),
-                    dst_ref=landing(slot, rows),
-                    send_sem=sent.at[index, k],
-                    recv_sem=arrived.at[index, k],
-                    device_id=(dest // width, dest % width),
-                    device_id_type=pl.DeviceIdType.MESH,
-                )
-
-            def wanted(device):
-                if reach is None:
-                    return [(None, extent)]
-                near = (device <= reach) | (device >= total - 1 - reach)
-                out = [(near, extent)]
-                if begin == 0:
-                    out.append(((device == own) & (own > reach), TILE))
-                return out
-
-            def guarded(condition, run):
-                if condition is None:
-                    run()
-                else:
-                    pl.when(condition)(run)
-
-            def one(k, carry):
-                dest = base + (slot + k) % size
-                if mode == "ends":
-                    source_ok = (me < reach) | (me >= total - reach)
-                    origin = (me - k + total) % total
-                    origin_ok = (origin < reach) | (origin >= total - reach)
-                    if action != "arrived":
-                        guarded(source_ok, lambda: getattr(move(k, dest, extent), "start" if action == "start" else "wait_send")())
-                    else:
-                        guarded(origin_ok, lambda: move(k, dest, extent).wait_recv())
-                    return carry
-                for condition, rows in wanted(me if action == "arrived" else dest):
-                    if action == "start":
-                        guarded(condition, lambda: move(k, dest, rows).start())
-                    elif action == "sent":
-                        guarded(condition, lambda: move(k, dest, rows).wait_send())
-                    else:
-                        guarded(condition, lambda: move(k, dest, rows).wait_recv())
-                return carry
-
-            if action == "start":
-                here = pltpu.make_async_copy(
-                    block(slot, extent), landing(slot, extent), local.at[index]
-                )
-                here.start()
-            lax.fori_loop(1, size, one, 0)
-            if action == "arrived":
-                pltpu.make_async_copy(
-                    block(slot, extent), landing(slot, extent), local.at[index]
-                ).wait()
-
-    copies("start")
-    copies("sent")
-    copies("arrived")
-
-
-def transfer(total, number, *jobs):
-    shapes, plans = [], []
-    for source, size, begin, extent, reach, mode in jobs:
-        dims = source.shape
-        if mode == "gather":
-            dims = (size,) + dims
-        elif extent is not None:
-            dims = dims[:2] + (extent,) + dims[3:]
-        shapes.append(jax.ShapeDtypeStruct(dims, source.dtype))
-        plans.append((size, begin, extent, reach, mode))
-    anywhere = pl.BlockSpec(memory_space=pl.ANY)
-    widest = max(plan[0] for plan in plans)
-    return pl.pallas_call(
-        functools.partial(transfer_kernel, total, tuple(plans)),
-        out_shape=shapes,
-        in_specs=[anywhere] * len(plans),
-        out_specs=[anywhere] * len(plans),
-        scratch_shapes=[
-            pltpu.SemaphoreType.DMA((len(plans), widest)),
-            pltpu.SemaphoreType.DMA((len(plans), widest)),
-            pltpu.SemaphoreType.DMA((len(plans),)),
-        ],
-        compiler_params=pltpu.CompilerParams(has_side_effects=True),
-        name=f"transfer{number}",
-    )(*[job[0] for job in jobs])
-
-
-def low_table(grid):
-    angles = np.arange(grid)[:, None] * np.arange(LOW // 2)[None, :]
-    cos_t, sin_t = turn(angles, grid)
-    return (np.concatenate([cos_t, -sin_t], 1) / grid).astype(np.float32)
-
-
-def force_rows(waves, rank):
-    total, _, _, rows = waves.shape
-    kx = np.arange(LOW) - LOW // 2
-    cos_l, sin_l = turn(np.arange(rows)[:, None] * kx[None, :], total * rows)
-    cos_s, sin_s = turn(np.arange(total)[:, None] * kx[None, :], total)
-    table = rotation(cos_l, -sin_l, (2, 0))
-    waves = contract("scnl,cldk->sdnk", waves, table)
-    real, imag = waves[:, 0], waves[:, 1]
-    c, s = (t.astype(np.float32)[:, None, :] for t in (cos_s, sin_s))
-    return jnp.stack([(real * c + imag * s).sum(0), (imag * c - real * s).sum(0)])
+def low_spectrum(grid_part, rank, total):
+    rows, grid = grid_part.shape
+    low = LOW // 2
+    cos_t, sin_t = turn(np.arange(grid)[:, None] * np.arange(low)[None, :], grid)
+    table = (np.concatenate([cos_t, -sin_t], 1) / grid).astype(np.float32)
+    waves = contract("xy,yn->xn", grid_part, table)
+    waves = jnp.stack([waves[:, :low], waves[:, low:]])
+    x = rank * rows + jnp.arange(rows, dtype=jnp.int32)
+    kx = jnp.arange(LOW, dtype=jnp.int32) - low
+    angle = ((kx[None, :] * x[:, None]) & (grid - 1)).astype(jnp.float32) * (2.0 * math.pi / grid)
+    c, s = jnp.cos(angle), jnp.sin(angle)
+    turns = jnp.stack([jnp.stack([c, -s]), jnp.stack([s, c])])
+    found = contract("cxn,cdxk->ndk", waves, turns)
+    return lax.psum(found, AXES)
 
 
 def body(vorticity_grid, forcing_grid, cutoff, forcing_shells):
@@ -914,13 +844,13 @@
     info = jnp.stack(
         [
             first_wave, extra_wave, (lane_rank == 0).astype(jnp.int32), half * (grid // 2),
-            cutoff[0], rank,
+            cutoff[0], rank, half * own,
         ]
     ).astype(jnp.int32)
     side = (1.0 - 2.0 * half.astype(jnp.float32)).reshape(1)
     y_forth, y_back = y_tables(grid, total, rows)
     x_forth, x_back, twist = x_tables(grid, total, rows)
-    y_forth, y_back = halves_of(y_forth), halves_of(y_back)
+    y_forth, y_back = stacked(y_forth), stacked(y_back)
     x_forth, x_back = halves_of(x_forth), halves_of(x_back)
     smem = pl.BlockSpec(memory_space=pltpu.SMEM)
     vmem = pl.BlockSpec(memory_space=pltpu.VMEM)
@@ -940,25 +870,26 @@
     start = pl.pallas_call(
         functools.partial(start_kernel, total, rows),
         out_shape=send_shape,
-        in_specs=[vmem] * 3,
+        in_specs=[vmem] * 2,
         out_specs=vmem,
         scratch_shapes=[waves_room, between],
         compiler_params=params(),
         name="start",
-    )(turned, *y_forth)
+    )(turned, y_forth)
 
     def product(*flat):
         return pl.pallas_call(
             functools.partial(product_kernel, total, rows, unit),
             out_shape=send_shape,
-            in_specs=[smem] + [vmem] * (4 + len(flat)),
+            in_specs=[smem] + [vmem] * (2 + len(flat)),
             out_specs=vmem,
             scratch_shapes=[
                 waves_room, scratch(total, rows, rows), scratch(total, rows, rows), between,
             ],
             compiler_params=params(),
+            cost_estimate=pl.CostEstimate(flops=10**10, bytes_accessed=0, transcendentals=0),
             name="product",
-        )(info, *y_forth, *y_back, *flat)
+        )(info, y_forth, y_back, *flat)
 
     def spectral(stage, source, *inputs):
         steps = rows // TILE + 1
@@ -993,17 +924,12 @@
             compiler_params=pltpu.CompilerParams(
                 vmem_limit_bytes=56 * 1024 * 1024, has_side_effects=True
             ),
+            cost_estimate=pl.CostEstimate(flops=10**10, bytes_accessed=0, transcendentals=0),
             name=f"spectral{stage}",
         )(info, side, source, *tables, *inputs)
 
     count_q = -(-half_low // total)
-    share = half_low // total
-    force = contract("xy,yn->nx", forcing_grid, low_table(grid))
-    force = force.reshape(2, total, share, rows).transpose(1, 0, 2, 3)
-    (force,) = transfer(total, 0, (force, total, 0, None, None, "all"))
-    force = force_rows(force, rank)
-    (force,) = transfer(total, 1, (force, total, 0, None, None, "gather"))
-    force = force.transpose(0, 2, 1, 3).reshape(half_low, 2, LOW)
+    force = low_spectrum(forcing_grid, rank, total)
     turned_force = jnp.roll(jnp.flip(force, 2), 1, 2) * jnp.array([1.0, -1.0])[None, :, None]
     turned_force = jnp.roll(jnp.flip(turned_force, 0), 1, 0)
     force_all = jnp.concatenate([turned_force, force], 0)
@@ -1029,12 +955,11 @@
     drive = jnp.concatenate([part[..., count_q:], gap, part[..., :count_q]], 3)
 
     state, fields = spectral(0, start)
-    own_start = lax.dynamic_slice_in_dim(start, half * own, own, 0)
-    advect = product(fields, own_start)
+    advect = product(fields, start)
     moved, first, fields = spectral(1, advect, state, drive)
     advect = product(fields)
     ahead, now = spectral(2, advect, state, moved, first, drive)
-    block = jnp.concatenate([ahead[..., rows - count_q :], ahead[..., :count_q]], -1)
+    block = ahead[..., : 2 * count_q]
     spectrum = now.transpose(1, 2, 3, 0).reshape(2, rows, grid)
 
     part_of = LOW // total
@@ -1047,7 +972,7 @@
     column = np.stack([np.stack([col_cos, col_sin]), np.stack([-col_sin, col_cos])])
     column = column.reshape(2, 2, 2 * count_q, total, LOW)
     mixed = contract("pctq,cdqpa->adt", block, column).reshape(total, part_of, 2, rows)
-    (mixed,) = transfer(total, 7, (mixed, total, 0, None, count_d, "ends"))
+    mixed = lax.all_to_all(mixed, AXES, split_axis=0, concat_axis=0, tiled=True)
     mixed = jnp.concatenate([mixed[total - count_d :], mixed[:count_d]], 0)
     mixed = mixed.transpose(2, 0, 3, 1).reshape(2, 2 * count_d * rows, part_of)
     coarse = contract("cqa,cqb->ab", mixed, np.stack([col_cos, -col_sin]))

time: 636 us -> 562 us (0.88)
  Pallas kernels: 561 us -> 481 us
  local copies, waits for them, and re-layouts: 48.9 us -> 31.1 us
  between operations: 9.18 us -> 22.7 us
  starting transfers between devices: 0 us -> 8.09 us
    pallas_call x2, Pallas kernels: 95.3 us -> 53.4 us  [product(): pl.pallas_call(functools.partial(product_kernel, total, rows, unit), out_...]
    pallas_call x3 -> x0, Pallas kernels: 40.1 us -> none  [transfer(): pl.pallas_call(functools.partial(transfer_kernel, total, tuple(plans)), o...]
    slice x3 -> x0, local copies, waits for them, and re-layouts: 14.5 us -> none  [the longest x2 11 us: body(): ahead[..., rows - count_q:]]
    all_to_all x0 -> x1, starting transfers between devices: none -> 8.05 us  [body(): mixed = lax.all_to_all(mixed, AXES, split_axis=0, concat_axis=0, tiled=True)]
  transfers between devices with their start and end apart: 0 -> 2, of which waited for: 0 -> 0; matrix products, arithmetic and copies ran while one was open for 0% -> 3% of each run, Pallas kernels for 0% -> 34%
where the time goes in v2:
time: 562 us; the launch traced here: 561 us
  Pallas kernels  481 us (86%)
  local copies, waits for them, and re-layouts  31.1 us (6%)
  between operations  22.7 us (4%)
  matrix products  11.6 us (2%)
  starting transfers between devices  8.09 us (1%)
  other arithmetic  6.24 us (1%)
    pallas_call x3, Pallas kernels, spectral(): pl.pallas_call(functools.partial(spectral_kernel, total, rows, grid, stag...  418 us
    pallas_call x2, Pallas kernels, product(): pl.pallas_call(functools.partial(product_kernel, total, rows, unit), out_...  53.4 us
    dot_general x4, matrix products, contract(): jnp.einsum(pattern, left_side, right_side, precision=lax.Precision.HIGH)  11.6 us
  transfers between devices with their start and end apart: 2, of which 0 were waited for; matrix products, arithmetic and copies ran while one was open for 3% of the time, Pallas kernels for 34%

profile of v2, /device:TPU:0, one launch (start us, length us, event | category | flops | bytes accessed | tf_op | source)
XLA Modules:
  0.0 561.0 jit_solution(16800767744599988602)
XLA Ops:
  7.2 0.0 copy-start
  7.2 0.0 all-reduce.2.cloned.1.call-start
  7.3 1.5 copy-done
  8.8 5.6 %convolution_bitcast_fusion.1 = f32[128,256]{0,1:T(8,128)S(1)} fusion(f32[4096,256]{1,0:T(8,128)} %constant.93.clone, f32[128,4096]{1,0:T(8,128)S(1)} %copy-done), kind=kOutput, calls=%fused_computation.7 | convolution fusion | flops 805306368 | bytes 6422528 | tf_op jit(solution)/shard_map/xy,yn->xn/dot_general | solution.py:22
  14.4 0.6 fusion.23
  15.0 1.0 convolution_bitcast_fusion
  16.0 0.0 all-reduce.2.cloned.1.call-update
  16.1 0.0 copy-done.3
  16.1 0.7 fusion.28
  25.2 1.9 copy.29
  27.1 2.6 copy.48
  29.6 9.7 %start.1.refs_2_.refs_1_ = f32[32,2,128,128]{3,2,1,0:T(8,128)} custom-call(f32[32,128,128]{2,1,0:T(8,128)} %bitcast.71, bf16[32,512,128]{2,1,0:T(8,128)(2,1)} %constant.92.clone.forth), custom_call_target="tpu_custom_call" | custom-call | tf_op jit(solution)/shard_map/start/pallas_call | solution.py:870
  39.3 0.7 stack.59.refs_0_.info
  40.0 154.0 %spectral0.1 = (f32[32,2,144,128]{3,2,1,0:T(8,128)}, f32[16,3,2,128,128]{4,3,2,1,0:T(8,128)}) custom-call(s32[7]{0:T(128)} %stack.59.refs_0_.info, f32[1]{0:T(128)} %bitcast.6.refs_1_, f32[32,2,128,128]{3,2,1,0:T(8,128)} %start.1.refs_2_.refs_1_, f32[32,2,1,128]{3,2,1,0:T(1,128)} %constant.95.clone.refs_3_, bf16[256,256]{1,0:T(8,128)(2,1)} %constant.96.clone.refs_4_, ...), custom_call_target="tpu_custom_call" | custom-call | flops 10000000000 | tf_op jit(solution)/shard_map/spectral0/pallas_call | solution.py:917
  194.0 0.0 copy-start.4
  194.0 27.0 %product.2.refs_2_ = f32[32,2,128,128]{3,2,1,0:T(8,128)} custom-call(s32[7]{0:T(128)} %stack.59.refs_0_.info, bf16[32,512,128]{2,1,0:T(8,128)(2,1)} %constant.92.clone.forth, bf16[32,256,256]{2,1,0:T(8,128)(2,1)} %constant.100.clone.back, f32[16,3,2,128,128]{4,3,2,1,0:T(8,128)} %get-tuple-element.9.refs_0_, f32[32,2,128,128]{3,2,1,0:T(8,128)} %start.1.refs_2_.refs_1_), custom_call_target="tpu_custom_call" | custom-call | flops 10000000000 | tf_op jit(solution)/shard_map/product/pallas_call | solution.py:881
  221.0 0.2 fusion.19
  221.2 0.1 pad.6.clone
  221.3 0.1 pad.3.clone
  221.4 0.0 all-reduce.2.cloned.1.call-done
  221.4 1.1 slice.86
  222.5 0.4 reverse.4
  222.8 0.1 slice.102
  223.0 0.9 slice.85
  223.9 0.0 copy-done.4
  223.9 0.1 maximum_multiply_fusion
  224.1 0.2 slice.76
  224.3 0.7 broadcast_select_fusion
  225.0 1.1 fusion.11
  226.1 0.1 pad_maximum_fusion.1
  226.2 0.2 copy.32
  226.4 2.9 copy.33
  229.3 5.5 fusion.26
  234.9 3.4 pad_maximum_fusion.refs_9_.refs_11_
  238.3 174.0 %spectral1.1 = (f32[32,2,144,128]{3,2,1,0:T(8,128)}, f32[32,2,144,128]{3,2,1,0:T(8,128)}, f32[16,4,2,128,128]{4,3,2,1,0:T(8,128)}) custom-call(s32[7]{0:T(128)} %stack.59.refs_0_.info, f32[1]{0:T(128)} %bitcast.6.refs_1_, f32[32,2,128,128]{3,2,1,0:T(8,128)} %product.2.refs_2_, f32[32,2,1,128]{3,2,1,0:T(1,128)} %constant.95.clone.refs_3_, ...), custom_call_target="tpu_custom_call" | custom-call | flops 10000000000 | tf_op jit(solution)/shard_map/spectral1/pallas_call | solution.py:917
  412.3 26.4 %product.3.refs_2_ = f32[32,2,128,128]{3,2,1,0:T(8,128)} custom-call(s32[7]{0:T(128)} %stack.59.refs_0_.info, bf16[32,512,128]{2,1,0:T(8,128)(2,1)} %constant.92.clone.forth, bf16[32,256,256]{2,1,0:T(8,128)(2,1)} %constant.100.clone.back, f32[16,4,2,128,128]{4,3,2,1,0:T(8,128)} %get-tuple-element.11.refs_0_), custom_call_target="tpu_custom_call" | custom-call | flops 10000000000 | tf_op jit(solution)/shard_map/product/pallas_call | solution.py:881
  438.6 90.2 %spectral2.1 = (f32[32,2,128,128]{3,2,1,0:T(8,128)}, f32[32,2,128,128]{3,2,1,0:T(8,128)}) custom-call(s32[7]{0:T(128)} %stack.59.refs_0_.info, f32[1]{0:T(128)} %bitcast.6.refs_1_, f32[32,2,128,128]{3,2,1,0:T(8,128)} %product.3.refs_2_, f32[32,2,1,128]{3,2,1,0:T(1,128)} %constant.95.clone.refs_3_, bf16[256,256]{1,0:T(8,128)(2,1)} %constant.96.clone.refs_4_, ...), custom_call_target="tpu_custom_call" | custom-call | flops 10000000000 | tf_op jit(solution)/shard_map/spectral2/pallas_call | solution.py:917
  528.9 0.0 copy-done.5
  528.9 4.2 fusion.3
  533.0 0.1 copy.36
  533.2 0.7 copy.37
  533.9 8.1 %all-to-all-start = ((f32[32,8,2,128]{3,1,2,0:T(8,128)}), f32[32,8,2,128]{3,1,2,0:T(8,128)S(1)}, u32[]{:S(2)}, u32[]{:S(2)}) async-start(f32[32,8,2,128]{3,1,2,0:T(8,128)} %copy.37), calls=%async_computation | async-start | bytes 524288 | tf_op jit(solution)/shard_map/all_to_all | solution.py:975
  542.0 5.6 copy.34
  547.5 5.8 %copy.39 = f32[2,128,4096]{2,1,0:T(8,128)} copy(f32[2,128,4096]{1,2,0:T(8,128)} %bitcast.70) | data formatting | bytes 8388608
  553.3 0.0 all-to-all-done
  553.3 0.0 copy-done.2
  553.3 0.8 convolution_bitcast_fusion.2
  554.1 0.0 copy-done.1
  (16 shorter events, 0.1 us)
Async XLA Ops:
  7.2 1.6 copy-start
  7.2 214.2 %all-reduce.2.cloned.1.call-start = ((), (), s32[]{:S(2)}) async-start(), calls=%async_computation.1 | async-start | bytes 524288 | tf_op jit(solution)/shard_map/psum | solution.py:830
  8.8 7.3 %copy-start.3 = (s32[4]{0:T(128)S(1)}, s32[4]{0:T(128)}, u32[]{:S(2)}) copy-start(s32[4]{0:T(128)} %param.18) | copy-start | bytes 52
  194.0 29.9 %copy-start.4 = (f32[2]{0:T(128)S(1)}, f32[2]{0:T(128)}, u32[]{:S(2)}) copy-start(f32[2]{0:T(128)} %constant.94.clone) | copy-start | bytes 28
  438.6 90.2 %copy-start.5 = (f32[2,2,8,32,256]{4,2,0,1,3:T(8,128)S(1)}, f32[2,2,8,32,256]{4,2,0,1,3:T(8,128)}, u32[]{:S(2)}) copy-start(f32[2,2,8,32,256]{4,2,0,1,3:T(8,128)} %constant.101.clone) | copy-start | bytes 3145732
  533.9 19.4 %all-to-all-start = ((f32[32,8,2,128]{3,1,2,0:T(8,128)}), f32[32,8,2,128]{3,1,2,0:T(8,128)S(1)}, u32[]{:S(2)}, u32[]{:S(2)}) async-start(f32[32,8,2,128]{3,1,2,0:T(8,128)} %copy.37), calls=%async_computation | async-start | bytes 524288 | tf_op jit(solution)/shard_map/all_to_all | solution.py:975
  547.5 6.6 %copy-start.1 = (f32[128,4096]{1,0:T(8,128)S(1)}, f32[128,4096]{1,0:T(8,128)}, u32[]{:S(2)}) copy-start(f32[128,4096]{1,0:T(8,128)} %param.16) | copy-start | bytes 6291460
  547.5 5.8 %copy-start.2 = (f32[2,256,256]{2,1,0:T(8,128)S(1)}, f32[2,256,256]{2,1,0:T(8,128)}, u32[]{:S(2)}) copy-start(f32[2,256,256]{2,1,0:T(8,128)} %constant.102.clone) | copy-start | bytes 1572868
Sparse Core Ops, SparseCore 0:
  16.2 150.7 all-reduce.1

commit v3 on v2

--- a/solution.py
+++ b/solution.py
@@ -74,7 +74,7 @@
 TILE = 16
 PART = 32
 GROUP = 4
-FLIGHT = 2
+FLIGHT = 4
 
 
 def plus(one, two, sign=1.0):

time: 562 us -> 557 us (level)
  no operation moved by 1% of the time
where the time goes in v3:
time: 557 us; the launch traced here: 556 us
  Pallas kernels  477 us (86%)
  local copies, waits for them, and re-layouts  31.1 us (6%)
  between operations  22.7 us (4%)
  matrix products  11.6 us (2%)
  starting transfers between devices  7.58 us (1%)
  other arithmetic  6.24 us (1%)
    pallas_call x3, Pallas kernels, spectral(): pl.pallas_call(functools.partial(spectral_kernel, total, rows, grid, stag...  414 us
    pallas_call x2, Pallas kernels, product(): pl.pallas_call(functools.partial(product_kernel, total, rows, unit), out_...  53.4 us
    dot_general x4, matrix products, contract(): jnp.einsum(pattern, left_side, right_side, precision=lax.Precision.HIGH)  11.6 us
  transfers between devices with their start and end apart: 2, of which 0 were waited for; matrix products, arithmetic and copies ran while one was open for 3% of the time, Pallas kernels for 34%

profile of v3, /device:TPU:0, one launch (start us, length us, event | category | flops | bytes accessed | tf_op | source)
XLA Modules:
  0.0 555.9 jit_solution(8141771789557909892)
XLA Ops:
  7.2 0.0 copy-start
  7.2 0.0 all-reduce.2.cloned.1.call-start
  7.3 1.5 copy-done
  8.8 5.6 %convolution_bitcast_fusion.1 = f32[128,256]{0,1:T(8,128)S(1)} fusion(f32[4096,256]{1,0:T(8,128)} %constant.93.clone, f32[128,4096]{1,0:T(8,128)S(1)} %copy-done), kind=kOutput, calls=%fused_computation.7 | convolution fusion | flops 805306368 | bytes 6422528 | tf_op jit(solution)/shard_map/xy,yn->xn/dot_general | solution.py:22
  14.4 0.6 fusion.23
  15.0 1.0 convolution_bitcast_fusion
  16.0 0.0 all-reduce.2.cloned.1.call-update
  16.1 0.0 copy-done.3
  16.1 0.7 fusion.28
  25.2 1.9 copy.29
  27.1 2.6 copy.48
  29.6 9.7 %start.1.refs_2_.refs_1_ = f32[32,2,128,128]{3,2,1,0:T(8,128)} custom-call(f32[32,128,128]{2,1,0:T(8,128)} %bitcast.71, bf16[32,512,128]{2,1,0:T(8,128)(2,1)} %constant.92.clone.forth), custom_call_target="tpu_custom_call" | custom-call | tf_op jit(solution)/shard_map/start/pallas_call | solution.py:870
  39.3 0.7 stack.59.refs_0_.info
  40.0 150.3 %spectral0.1 = (f32[32,2,144,128]{3,2,1,0:T(8,128)}, f32[16,3,2,128,128]{4,3,2,1,0:T(8,128)}) custom-call(s32[7]{0:T(128)} %stack.59.refs_0_.info, f32[1]{0:T(128)} %bitcast.6.refs_1_, f32[32,2,128,128]{3,2,1,0:T(8,128)} %start.1.refs_2_.refs_1_, f32[32,2,1,128]{3,2,1,0:T(1,128)} %constant.95.clone.refs_3_, bf16[256,256]{1,0:T(8,128)(2,1)} %constant.96.clone.refs_4_, ...), custom_call_target="tpu_custom_call" | custom-call | flops 10000000000 | tf_op jit(solution)/shard_map/spectral0/pallas_call | solution.py:917
  190.3 0.0 copy-start.4
  190.3 27.0 %product.2.refs_2_ = f32[32,2,128,128]{3,2,1,0:T(8,128)} custom-call(s32[7]{0:T(128)} %stack.59.refs_0_.info, bf16[32,512,128]{2,1,0:T(8,128)(2,1)} %constant.92.clone.forth, bf16[32,256,256]{2,1,0:T(8,128)(2,1)} %constant.100.clone.back, f32[16,3,2,128,128]{4,3,2,1,0:T(8,128)} %get-tuple-element.9.refs_0_, f32[32,2,128,128]{3,2,1,0:T(8,128)} %start.1.refs_2_.refs_1_), custom_call_target="tpu_custom_call" | custom-call | flops 10000000000 | tf_op jit(solution)/shard_map/product/pallas_call | solution.py:881
  217.3 0.2 fusion.19
  217.5 0.1 pad.6.clone
  217.6 0.1 pad.3.clone
  217.7 0.0 all-reduce.2.cloned.1.call-done
  217.7 1.1 slice.86
  218.8 0.4 reverse.4
  219.2 0.1 slice.102
  219.3 0.9 slice.85
  220.2 0.0 copy-done.4
  220.2 0.1 maximum_multiply_fusion
  220.4 0.2 slice.76
  220.6 0.7 broadcast_select_fusion
  221.3 1.1 fusion.11
  222.4 0.1 pad_maximum_fusion.1
  222.5 0.2 copy.32
  222.7 2.9 copy.33
  225.7 5.5 fusion.26
  231.2 3.4 pad_maximum_fusion.refs_9_.refs_11_
  234.6 170.1 %spectral1.1 = (f32[32,2,144,128]{3,2,1,0:T(8,128)}, f32[32,2,144,128]{3,2,1,0:T(8,128)}, f32[16,4,2,128,128]{4,3,2,1,0:T(8,128)}) custom-call(s32[7]{0:T(128)} %stack.59.refs_0_.info, f32[1]{0:T(128)} %bitcast.6.refs_1_, f32[32,2,128,128]{3,2,1,0:T(8,128)} %product.2.refs_2_, f32[32,2,1,128]{3,2,1,0:T(1,128)} %constant.95.clone.refs_3_, ...), custom_call_target="tpu_custom_call" | custom-call | flops 10000000000 | tf_op jit(solution)/shard_map/spectral1/pallas_call | solution.py:917
  404.7 26.4 %product.3.refs_2_ = f32[32,2,128,128]{3,2,1,0:T(8,128)} custom-call(s32[7]{0:T(128)} %stack.59.refs_0_.info, bf16[32,512,128]{2,1,0:T(8,128)(2,1)} %constant.92.clone.forth, bf16[32,256,256]{2,1,0:T(8,128)(2,1)} %constant.100.clone.back, f32[16,4,2,128,128]{4,3,2,1,0:T(8,128)} %get-tuple-element.11.refs_0_), custom_call_target="tpu_custom_call" | custom-call | flops 10000000000 | tf_op jit(solution)/shard_map/product/pallas_call | solution.py:881
  431.1 93.2 %spectral2.1 = (f32[32,2,128,128]{3,2,1,0:T(8,128)}, f32[32,2,128,128]{3,2,1,0:T(8,128)}) custom-call(s32[7]{0:T(128)} %stack.59.refs_0_.info, f32[1]{0:T(128)} %bitcast.6.refs_1_, f32[32,2,128,128]{3,2,1,0:T(8,128)} %product.3.refs_2_, f32[32,2,1,128]{3,2,1,0:T(1,128)} %constant.95.clone.refs_3_, bf16[256,256]{1,0:T(8,128)(2,1)} %constant.96.clone.refs_4_, ...), custom_call_target="tpu_custom_call" | custom-call | flops 10000000000 | tf_op jit(solution)/shard_map/spectral2/pallas_call | solution.py:917
  524.3 0.0 copy-done.5
  524.3 4.2 fusion.3
  528.5 0.1 copy.36
  528.6 0.7 copy.37
  529.3 7.5 %all-to-all-start = ((f32[32,8,2,128]{3,1,2,0:T(8,128)}), f32[32,8,2,128]{3,1,2,0:T(8,128)S(1)}, u32[]{:S(2)}, u32[]{:S(2)}) async-start(f32[32,8,2,128]{3,1,2,0:T(8,128)} %copy.37), calls=%async_computation | async-start | bytes 524288 | tf_op jit(solution)/shard_map/all_to_all | solution.py:975
  536.9 5.6 %copy.34 = f32[2,128,128,32]{1,3,2,0:T(8,128)} copy(f32[2,128,128,32]{2,1,0,3:T(8,128)} %bitcast.73) | data formatting | bytes 8388608 | tf_op jit(solution)/shard_map/transpose | solution.py:963
  542.4 5.8 %copy.39 = f32[2,128,4096]{2,1,0:T(8,128)} copy(f32[2,128,4096]{1,2,0:T(8,128)} %bitcast.70) | data formatting | bytes 8388608
  548.2 0.0 all-to-all-done
  548.2 0.0 copy-done.2
  548.2 0.8 convolution_bitcast_fusion.2
  549.1 0.0 copy-done.1
  (16 shorter events, 0.1 us)
Async XLA Ops:
  7.2 1.6 copy-start
  7.2 210.5 %all-reduce.2.cloned.1.call-start = ((), (), s32[]{:S(2)}) async-start(), calls=%async_computation.1 | async-start | bytes 524288 | tf_op jit(solution)/shard_map/psum | solution.py:830
  8.8 7.3 %copy-start.3 = (s32[4]{0:T(128)S(1)}, s32[4]{0:T(128)}, u32[]{:S(2)}) copy-start(s32[4]{0:T(128)} %param.18) | copy-start | bytes 52
  190.3 30.0 %copy-start.4 = (f32[2]{0:T(128)S(1)}, f32[2]{0:T(128)}, u32[]{:S(2)}) copy-start(f32[2]{0:T(128)} %constant.94.clone) | copy-start | bytes 28
  431.1 93.2 %copy-start.5 = (f32[2,2,8,32,256]{4,2,0,1,3:T(8,128)S(1)}, f32[2,2,8,32,256]{4,2,0,1,3:T(8,128)}, u32[]{:S(2)}) copy-start(f32[2,2,8,32,256]{4,2,0,1,3:T(8,128)} %constant.101.clone) | copy-start | bytes 3145732
  529.3 18.9 %all-to-all-start = ((f32[32,8,2,128]{3,1,2,0:T(8,128)}), f32[32,8,2,128]{3,1,2,0:T(8,128)S(1)}, u32[]{:S(2)}, u32[]{:S(2)}) async-start(f32[32,8,2,128]{3,1,2,0:T(8,128)} %copy.37), calls=%async_computation | async-start | bytes 524288 | tf_op jit(solution)/shard_map/all_to_all | solution.py:975
  542.4 6.6 %copy-start.1 = (f32[128,4096]{1,0:T(8,128)S(1)}, f32[128,4096]{1,0:T(8,128)}, u32[]{:S(2)}) copy-start(f32[128,4096]{1,0:T(8,128)} %param.16) | copy-start | bytes 6291460
  542.4 5.8 %copy-start.2 = (f32[2,256,256]{2,1,0:T(8,128)S(1)}, f32[2,256,256]{2,1,0:T(8,128)}, u32[]{:S(2)}) copy-start(f32[2,256,256]{2,1,0:T(8,128)} %constant.102.clone) | copy-start | bytes 1572868
Sparse Core Ops, SparseCore 0:
  16.2 152.1 all-reduce.1
